TPU v7x, 32 devices: a whole 2x2x4 slice. The times are simulated.
32 devices in a mesh: groups: 2 (over y), tp: 4 (over z), seq: 4 (over x, core).
Axes of the slice: x: 2, y: 2, z: 4, core: 2. Of those that a mesh axis runs over, the one named last changes fastest.
Arguments:
- kv_prefill: bfloat16 [2, 2, 8, 32768, 128], P(None, None, 'groups', ('tp', 'seq')), parts along dimension 2, may hold values from -10 to 10
- queries: bfloat16 [2, 8, 64, 128], P(None, ('groups', 'seq'), 'tp'), parts along dimension 1, may hold values from -512 to 512
- new_kv: bfloat16 [2, 2, 8, 8, 128], P(None, None, ('groups', 'seq')), parts along dimension 2, may hold values from -4.5 to 4.5
- lengths: int32 [8], P(('groups', 'seq')), parts along dimension 0, may hold values from 2048 to 4095
- page_slots: int32 [8, 256], P(('groups', 'seq')), parts along dimension 0, may hold values from 0 to 255, each once within a row
Outputs:
- decode_pool: bfloat16 [2, 2, 8, 2048, 16, 128], P(None, None, 'tp', ('groups', 'seq')), parts along dimension 3
- attention_out: bfloat16 [2, 8, 64, 128], P(None, ('groups', 'seq'), 'tp'), parts along dimension 1
There are 2 independent parts, one for each index of `groups`. A program takes and returns all parts, laid end to end along the dimension named above; each array names one. Nothing has to cross between parts.
Inputs may be any that keep to these rules, and one draw needn't show every extreme that they name: Row b belongs to sequence b: its page j goes to slot page_slots[b, j] of the row's block of 256 slots; each row uses every slot once.
All inputs are finite; a program needn't handle non-finite values.
Results may differ from a plain program's by a relative error of at most 0.01.
Values may be sent and summed in bfloat16 or wider, within the bound.
A program may use at most 64 MiB of HBM per device.

v0:
```python
import math

import jax
import jax.numpy as jnp
from jax import lax
from jax.sharding import PartitionSpec as P

KVH = 8
PAGE = 16
CTX = 4096


def swapped(array, axis, bit):
    return lax.ppermute(array, axis, [(i, i ^ 1 << bit) for i in range(lax.axis_size(axis))])


def spread_heads(blocks, axis_dim):
    tp_ranks = lax.axis_size("tp")
    kv_rank = max(1, KVH // tp_ranks)
    fanout = tp_ranks * kv_rank // KVH
    levels = fanout.bit_length() - 1
    ordering = list(range(levels))
    my_rank = lax.axis_index("tp")
    finished = []
    for bit_index in ordering:
        partner = swapped(blocks, "tp", bit_index)
        lower_side = my_rank // (1 << bit_index) % 2 == 0
        lower_part = jnp.where(lower_side, blocks, partner)
        upper_part = jnp.where(lower_side, partner, blocks)
        higher_bits = sum((1 for earlier in finished if earlier > bit_index))
        shape_now = blocks.shape
        outer_count = 2**higher_bits
        split_shape = (
            shape_now[:axis_dim]
            + (outer_count, shape_now[axis_dim] // outer_count)
            + shape_now[axis_dim + 1 :]
        )
        paired = jnp.stack(
            (lower_part.reshape(split_shape), upper_part.reshape(split_shape)), axis=axis_dim + 1
        )
        blocks = paired.reshape(
            shape_now[:axis_dim] + (2 * shape_now[axis_dim],) + shape_now[axis_dim + 1 :]
        )
        finished.append(bit_index)
    return blocks


def repack(grouped, page_row, local_seqs):
    layers_here = grouped.shape[1]
    head_count = grouped.shape[3] // CTX
    head_dim = grouped.shape[4]
    paged_rows = grouped.reshape(
        2, layers_here, local_seqs, head_count, CTX // PAGE, PAGE, head_dim
    )
    paged_rows = paged_rows.transpose(0, 1, 3, 2, 4, 5, 6).reshape(
        2, layers_here, head_count, local_seqs * (CTX // PAGE), PAGE, head_dim
    )
    inverse = jnp.argsort(page_row)
    return jnp.take(paged_rows, inverse, axis=3)


def body(kv_prefill, queries, new_kv, lengths, page_slots):
    local_seqs = lengths.shape[0]
    page_row = page_slots[0]
    tp_ranks = lax.axis_size("tp")
    kv_rank = max(1, KVH // tp_ranks)
    layer_count = kv_prefill.shape[1]
    grouped = spread_heads(kv_prefill, 3)
    block_rows = kv_prefill.shape[3]
    fanout = grouped.shape[3] // block_rows
    shaped = grouped.reshape(
        2, layer_count, grouped.shape[2], fanout, 1, block_rows, grouped.shape[4]
    )
    pieces = lax.all_to_all(shaped, "seq", split_axis=2, concat_axis=4, tiled=True)
    flattened = pieces.reshape(
        2,
        pieces.shape[1],
        pieces.shape[2],
        pieces.shape[3] * pieces.shape[4] * pieces.shape[5],
        pieces.shape[6],
    )
    decode_pool = repack(flattened, page_row, local_seqs)
    first_head = lax.axis_index("tp") * KVH // tp_ranks
    fresh_rows = lax.dynamic_slice_in_dim(new_kv, first_head, kv_rank, 3)
    pages_per = CTX // PAGE
    length_now = lengths[0]
    slot_now = lax.dynamic_index_in_dim(page_row, 0 + length_now // PAGE, 0, False)
    update = fresh_rows[:, :, 0][:, :, :, None, None, :]
    decode_pool = lax.dynamic_update_slice(
        decode_pool, update, (0, 0, 0, slot_now, length_now % PAGE, 0)
    )
    slot_table = page_row.reshape(local_seqs, pages_per)
    head_dim = queries.shape[3]
    key_cache = jnp.take(decode_pool[0], slot_table, axis=2).reshape(
        layer_count, kv_rank, local_seqs, CTX, head_dim
    )
    values = jnp.take(decode_pool[1], slot_table, axis=2).reshape(
        layer_count, kv_rank, local_seqs, CTX, head_dim
    )
    grouped_q = queries.reshape(
        layer_count, local_seqs, kv_rank, queries.shape[2] // kv_rank, head_dim
    )
    scores = jnp.einsum(
        "lskgd,lkstd->lskgt", grouped_q, key_cache, preferred_element_type=jnp.float32
    ) * (1.0 / math.sqrt(head_dim))
    positions = jnp.arange(CTX, dtype=jnp.int32)
    visible = (positions[None, :] <= lengths[:, None])[None, :, None, None, :]
    masked = jnp.where(visible, scores, -1e30)
    highest = jnp.max(masked, axis=-1, keepdims=True)
    exponent = jnp.where(visible, jnp.exp(masked - highest), 0.0)
    weights = (exponent / jnp.sum(exponent, axis=-1, keepdims=True)).astype(jnp.bfloat16)
    mixed_out = jnp.einsum(
        "lskgt,lkstd->lskgd", weights, values, preferred_element_type=jnp.float32
    )
    attention_out = mixed_out.astype(jnp.bfloat16).reshape(queries.shape)
    return (decode_pool, attention_out)


def solution(mesh):
    placed = (
        P(None, None, "groups", ("tp", "seq"), None),
        P(None, ("groups", "seq"), "tp", None),
        P(None, None, ("groups", "seq"), None, None),
        P(("groups", "seq")),
        P(("groups", "seq"), None),
    )
    return jax.shard_map(
        body,
        mesh=mesh,
        in_specs=placed,
        out_specs=(
            P(None, None, "tp", ("groups", "seq"), None, None),
            P(None, ("groups", "seq"), "tp", None),
        ),
        check_vma=False,
    )
```

profile of v0, /device:TPU:0, one launch (start us, length us, event | category | flops | bytes accessed | tf_op | source)
XLA Modules:
  0.0 178.7 jit_solution(6032146708819677429)
XLA Ops:
  0.6 0.0 copy-start
  0.6 7.6 %copy.21 = bf16[2,2,4,2048,128]{4,3,1,0,2:T(8,128)(2,1)} copy(bf16[2,2,4,2048,128]{4,3,2,1,0:T(8,128)(2,1)} %param.7) | data formatting | bytes 16777216 | tf_op args[0]
  8.2 0.0 copy-start.1
  8.2 5.8 %all-to-all-start = ((bf16[2,2,4,1,1,2048,128]{6,5,1,0,4,3,2:T(8,128)(2,1)}), bf16[2,2,4,1,1,2048,128]{6,5,1,0,4,3,2:T(8,128)(2,1)}, u32[]{:S(2)}, u32[]{:S(2)}) async-start(bf16[2,2,4,1,1,2048,128]{6,5,1,0,4,3,2:T(8,128)(2,1)} %bitcast.47), calls=%async_computation | async-start | bytes 16777216 | tf_op jit(solution)/shard_map/all_to_all | solution.py:74
  14.7 0.0 copy-done.1
  14.7 0.6 constant_dynamic-slice_fusion
  16.6 0.7 dynamic-slice_bitcast_fusion
  18.0 3.2 %sort.17 = (s32[256]{0:T(256)}, s32[256]{0:T(256)S(1)}) sort(s32[256]{0:T(256)S(1)} %bitcast.52, s32[256]{0:T(256)S(1)} %iota.10), dimensions={0}, to_apply=%region_0.0 | sort | flops 2048 | bytes 4096 | tf_op jit(solution)/shard_map/jit(argsort)/sort | solution.py:58
  21.3 86.6 %all-to-all-done = bf16[2,2,4,1,1,2048,128]{6,5,1,0,4,3,2:T(8,128)(2,1)} async-done(((bf16[2,2,4,1,1,2048,128]{6,5,1,0,4,3,2:T(8,128)(2,1)}), bf16[2,2,4,1,1,2048,128]{6,5,1,0,4,3,2:T(8,128)(2,1)}, u32[]{:S(2)}, u32[]{:S(2)}) %all-to-all-start) | async-done | bytes 8388640 | tf_op jit(solution)/shard_map/all_to_all | solution.py:74
  107.8 7.6 %copy.14 = bf16[2,2,4,1,1,2048,128]{6,5,2,1,0,4,3:T(8,128)(2,1)} copy(bf16[2,2,4,1,1,2048,128]{6,5,1,0,4,3,2:T(8,128)(2,1)} %all-to-all-done) | data formatting | bytes 16777216 | tf_op jit(solution)/shard_map/all_to_all | solution.py:74
  115.4 12.5 %gather_fusion = bf16[256,2,2,2,16,128]{5,4,3,2,1,0:T(8,128)(2,1)} fusion(bf16[2,2,2,256,16,128]{5,4,3,2,1,0:T(8,128)(2,1)} %bitcast.48, s32[1024]{0:T(1024)S(1)} %pad_clamp_fusion.1), kind=kCustom, calls=%fused_computation.2 | custom fusion | bytes 16778240 | tf_op jit(solution)/shard_map/jit(_take)/gather | solution.py:59
  127.9 7.4 %select_bitcast_fusion = bf16[2,2,2,256,16,128]{5,4,2,1,0,3:T(8,128)(2,1)} fusion(bf16[256,2,2,2,16,128]{5,4,3,2,1,0:T(8,128)(2,1)} %gather_fusion, pred[256]{0:T(512)(128)(4,1)S(1)} %compare_and_fusion), kind=kLoop, calls=%fused_computation.5 | loop fusion | flops 4194304 | bytes 16777472 | tf_op jit(solution)/shard_map/jit(_take)/select_n | solution.py:59
  135.4 1.3 dynamic_update_slice.3
  136.7 6.5 %slice_bitcast_fusion.1 = (bf16[2,2,256,16,128]{4,3,1,0,2:T(8,128)(2,1)}, bf16[2,2,256,16,128]{4,3,1,0,2:T(8,128)(2,1)}) fusion(bf16[2,2,2,256,16,128]{5,4,2,1,0,3:T(8,128)(2,1)} %dynamic_update_slice.3), kind=kLoop, calls=%fused_computation.13 | loop fusion | bytes 16777216 | tf_op jit(solution)/shard_map/squeeze | solution.py:94
  143.2 8.3 %copy.18 = bf16[2,2,2,256,16,128]{5,4,3,2,1,0:T(8,128)(2,1)} copy(bf16[2,2,2,256,16,128]{5,4,2,1,0,3:T(8,128)(2,1)} %dynamic_update_slice.3) | data formatting | bytes 16777216
  151.5 5.2 %gather_fusion.1 = bf16[256,2,2,16,128]{4,3,2,1,0:T(8,128)(2,1)} fusion(bf16[2,2,256,16,128]{4,3,1,0,2:T(8,128)(2,1)} %get-tuple-element.13, s32[1024]{0:T(1024)S(1)} %pad_clamp_fusion), kind=kCustom, calls=%fused_computation.clone | custom fusion | bytes 8389632 | tf_op jit(solution)/shard_map/jit(_take)/gather | solution.py:94
  156.7 5.2 %gather_fusion.2 = bf16[256,2,2,16,128]{4,3,2,1,0:T(8,128)(2,1)} fusion(bf16[2,2,256,16,128]{4,3,1,0,2:T(8,128)(2,1)} %get-tuple-element.14, s32[1024]{0:T(1024)S(1)} %pad_clamp_fusion), kind=kCustom, calls=%fused_computation.1.clone | custom fusion | bytes 8389632 | tf_op jit(solution)/shard_map/jit(_take)/gather | solution.py:97
  162.0 4.3 %bitcast_select_fusion.1 = (bf16[2,2,1,256,16,128]{5,4,1,0,3,2:T(8,128)(2,1)S(1)}, bf16[2,2,1,256,16,128]{5,4,1,0,3,2:T(8,128)(2,1)S(1)}) fusion(bf16[256,2,2,16,128]{4,3,2,1,0:T(8,128)(2,1)} %gather_fusion.1, pred[256]{0:T(512)(128)(4,1)S(1)} %get-tuple-element.11, bf16[256,2,2,16,128]{4,3,2,1,0:T(8,128)(2,1)} %gather_fusion.2), kind=kLoop, calls=%fused_computation.15 | loop fusion | flops 4194304 | bytes 16777472 | tf_op jit(solution)/shard_map/jit(_take)/select_n | solution.py:94
  166.3 2.7 %copy.16 = bf16[2,2,1,256,16,128]{5,4,3,1,0,2:T(8,128)(2,1)} copy(bf16[2,2,1,256,16,128]{5,4,1,0,3,2:T(8,128)(2,1)S(1)} %get-tuple-element.15) | data formatting | bytes 8388608 | tf_op jit(solution)/shard_map/jit(_take)/select_n | solution.py:94
  168.9 2.6 %copy.17 = bf16[2,2,1,256,16,128]{5,4,3,1,0,2:T(8,128)(2,1)} copy(bf16[2,2,1,256,16,128]{5,4,1,0,3,2:T(8,128)(2,1)S(1)} %get-tuple-element.16) | data formatting | bytes 8388608 | tf_op jit(solution)/shard_map/jit(_take)/select_n | solution.py:97
  171.6 0.0 copy-done
  171.6 3.6 %fusion.9 = (f32[2,2,8]{2,1,0:T(2,128)S(1)}, f32[2,2,8,4096]{3,2,1,0:T(8,128)S(1)}) fusion(pred[4096]{0:T(1024)(128)(4,1)S(1)} %iota_compare_fusion, bf16[2,2,4096,128]{3,2,1,0:T(8,128)(2,1)} %bitcast.49, bf16[2,1,16,128]{3,2,1,0:T(8,128)(2,1)S(1)} %copy-done), kind=kOutput, calls=%fused_computation.30 | convolution fusion | flops 34213888 | bytes 4731008 | tf_op jit(solution)/shard_map/sub | solution.py:110
  175.2 3.5 %fusion.6 = bf16[2,1,16,128]{3,2,1,0:T(8,128)(2,1)} fusion(bf16[2,2,4096,128]{3,2,1,0:T(8,128)(2,1)} %bitcast.50, f32[2,2,8,4096]{3,2,1,0:T(8,128)S(1)} %get-tuple-element.18, f32[2,2,8]{2,1,0:T(2,128)S(1)} %get-tuple-element.17), kind=kOutput, calls=%fused_computation.17 | convolution fusion | flops 33820672 | bytes 4726912 | tf_op jit(solution)/shard_map/lskgt,lkstd->lskgd/dot_general | solution.py:112
  (8 shorter events, 0.1 us)
Async XLA Ops:
  0.6 171.0 %copy-start = (bf16[2,1,16,128]{3,2,1,0:T(8,128)(2,1)S(1)}, bf16[2,1,16,128]{3,2,1,0:T(8,128)(2,1)}, u32[]{:S(2)}) copy-start(bf16[2,1,16,128]{3,2,1,0:T(8,128)(2,1)} %param.8) | copy-start | bytes 24580
  8.2 6.5 %copy-start.1 = (s32[1,256]{1,0:T(1,128)S(1)}, s32[1,256]{1,0:T(1,128)}, u32[]{:S(2)}) copy-start(s32[1,256]{1,0:T(1,128)} %param.11) | copy-start | bytes 3076
  8.2 99.6 %all-to-all-start = ((bf16[2,2,4,1,1,2048,128]{6,5,1,0,4,3,2:T(8,128)(2,1)}), bf16[2,2,4,1,1,2048,128]{6,5,1,0,4,3,2:T(8,128)(2,1)}, u32[]{:S(2)}, u32[]{:S(2)}) async-start(bf16[2,2,4,1,1,2048,128]{6,5,1,0,4,3,2:T(8,128)(2,1)} %bitcast.47), calls=%async_computation | async-start | bytes 16777216 | tf_op jit(solution)/shard_map/all_to_all | solution.py:74
where the time goes:
time: 179 us
  waiting for transfers between devices  86.6 us (48%)
  local copies, waits for them, and re-layouts  60.9 us (34%)
  other arithmetic  14.9 us (8%)
  matrix products  7.1 us (4%)
  starting transfers between devices  5.79 us (3%)
  between operations  3.37 us (2%)
    all_to_all x1, waiting for transfers between devices, body(): lax.all_to_all(shaped, 'seq', split_axis=2, concat_axis=4, tiled=True)  86.6 us
    unnamed x6, local copies, waits for them, and re-layouts  15.9 us
    gather x1, local copies, waits for them, and re-layouts, repack(): return jnp.take(paged_rows, inverse, axis=3)  12.5 us
    all_to_all x1, local copies, waits for them, and re-layouts, body(): lax.all_to_all(shaped, 'seq', split_axis=2, concat_axis=4, tiled=True)  7.59 us
    select_n x2, other arithmetic, repack(): return jnp.take(paged_rows, inverse, axis=3)  7.44 us
    squeeze x1, local copies, waits for them, and re-layouts, body(): decode_pool[0]  6.48 us
    all_to_all x1, starting transfers between devices, body(): lax.all_to_all(shaped, 'seq', split_axis=2, concat_axis=4, tiled=True)  5.79 us
    gather x1, local copies, waits for them, and re-layouts, body(): jnp.take(decode_pool[1], slot_table, axis=2)  5.25 us
  transfers between devices with their start and end apart: 1, of which 1 were waited for; matrix products, arithmetic and copies ran while one was open for 3% of the time, Pallas kernels for 0%

commit v1 on v0

v1 whole, which is shorter than its diff:
```python
import functools
import math

import jax
import jax.numpy as jnp
from jax import lax
from jax.experimental import pallas as pl
from jax.experimental.pallas import tpu as pltpu
from jax.sharding import PartitionSpec as P


PAGE = 16
UNROLL = 16


def swapped(array, axis, bits):
    return lax.ppermute(array, axis, [(i, i ^ bits) for i in range(lax.axis_size(axis))])


def spread_heads(blocks, fanout):
    rank = lax.axis_index("tp")
    for bit in range(fanout.bit_length() - 1):
        partner = swapped(blocks, "tp", 1 << bit)
        lower = rank // (1 << bit) % 2 == 0
        pair = (jnp.where(lower, blocks, partner), jnp.where(lower, partner, blocks))
        blocks = jnp.concatenate(pair, axis=3)
    return blocks


def cut_kernel(wanted, *refs):
    spread, outs, sems = refs[0], refs[-1 - len(wanted) : -1], refs[-1]
    me = lax.axis_index("seq")
    copies = []
    for out, items in zip(outs, wanted):
        for n, (k, l, delta, lo, hi) in enumerate(items):
            source = spread.at[k, l, me ^ delta, :, lo:hi]
            copies.append(pltpu.make_async_copy(source, out.at[n], sems.at[len(copies)]))
            copies[-1].start()
    for copy in copies:
        copy.wait()


def cut(spread, wanted, after):
    fanout, _, page, depth = spread.shape[3:]
    shapes = [
        jax.ShapeDtypeStruct((len(w), fanout, w[0][4] - w[0][3], page, depth), spread.dtype)
        for w in wanted
    ]
    anywhere = pl.BlockSpec(memory_space=pl.ANY)
    return pl.pallas_call(
        functools.partial(cut_kernel, wanted),
        out_shape=shapes,
        in_specs=[pl.BlockSpec(memory_space=pltpu.HBM)] + [anywhere] * len(after),
        out_specs=[pl.BlockSpec(memory_space=pltpu.VMEM)] * len(shapes),
        scratch_shapes=[pltpu.SemaphoreType.DMA((sum(len(w) for w in wanted),))],
        compiler_params=pltpu.CompilerParams(vmem_limit_bytes=8 << 20),
        cost_estimate=pl.CostEstimate(
            flops=0, bytes_accessed=2 * sum(2 * math.prod(o.shape) for o in shapes), transcendentals=0
        ),
    )(spread, *after)


def head_kernel(plan, *refs):
    refs = list(refs)

    def take(count):
        return [refs.pop(0) for _ in range(count)]

    units, group, sources = plan["units"], plan["group"], plan["sources"]
    slots, lengths, queries, fresh = take(4)
    own_ref = take(1)[0] if plan["own"] else None
    operands = take(plan["operands"])
    given_probs = dict(zip(plan["given_probs"], take(len(plan["given_probs"]))))
    sums_in = dict(zip(plan["sums_in"], take(len(plan["sums_in"]))))
    if plan["has_pool"]:
        take(1)
    (pool,) = take(1)
    probs_out = dict(zip(plan["probs_out"], take(len(plan["probs_out"]))))
    sums_out = dict(zip(plan["sums_out"], take(len(plan["sums_out"]))))
    attention_out = take(1)[0] if plan["final"] else None
    scores, paged, own_buf, in_sems, out_sems = refs

    me = lax.axis_index("seq")
    mine = me % sources
    head = (me // sources) ^ group
    heads = plan["heads"]
    first = lax.axis_index("tp") * plan["kv_heads"] // plan["tp_ranks"]
    fanout, blocks, _, depth = plan["piece"]
    length = lengths[0]
    per_head = queries.shape[2]
    places = lax.broadcasted_iota(jnp.int32, scores.shape, 0) * (blocks * PAGE)
    places += lax.broadcasted_iota(jnp.int32, scores.shape, 2)
    fetches = []
    if plan["own"]:
        for n, (k, l) in enumerate(units):
            fetches.append(
                pltpu.make_async_copy(own_ref.at[k, l, me], own_buf.at[n], in_sems.at[n])
            )
            fetches[-1].start()

    probs_now = dict(given_probs)
    sums = dict(sums_in)
    flushes = []
    for n, (k, l) in enumerate(units):
        parts = []
        if plan["own"]:
            fetches[n].wait()
            parts.append((own_buf.at[n], 0, 0, blocks))
        parts += [
            (operands[at].at[row], e, lo, hi)
            for at, row, unit, e, lo, hi in plan["parts"]
            if unit == (k, l)
        ]
        rows = fresh[k, l, 0].astype(jnp.float32)
        row_at = lax.broadcasted_iota(jnp.int32, rows.shape, 0)
        row = jnp.sum(jnp.where(row_at == first + head, rows, 0.0), axis=0, keepdims=True)

        def patched(page):
            offset = lax.broadcasted_iota(jnp.int32, page.shape, 0)
            return jnp.where(offset == length % PAGE, row, page.astype(jnp.float32)).astype(page.dtype)

        if plan["close"]:
            count = 0
            for ref, e, lo, hi in parts:
                for f in range(fanout):
                    base = (f * sources + (mine ^ e)) * blocks + lo
                    paged[n, count : count + hi - lo] = ref[f]
                    inside = (length // PAGE >= base) & (length // PAGE < base + hi - lo)

                    @pl.when(inside)
                    def _():
                        at = count + length // PAGE - base
                        paged[n, at] = patched(paged[n, at])

                    for b in range(hi - lo):
                        pltpu.make_async_copy(
                            paged.at[n, count + b],
                            pool.at[k, l, head, slots[0, base + b]],
                            out_sems.at[n],
                        ).start()
                    count += hi - lo
            done = pltpu.make_async_copy(
                paged.at[n, :count], pool.at[k, l, head, :count], out_sems.at[n]
            )
        else:
            for ref, e, lo, hi in parts:
                for f in range(fanout):
                    base = (f * sources + (mine ^ e)) * blocks + lo
                    unroll = math.gcd(UNROLL, hi - lo)

                    def move(step, carry, ref=ref, f=f, base=base, unroll=unroll):
                        start = step * unroll
                        held = [ref[f, start + i] for i in range(unroll)]
                        for i in range(unroll):
                            paged[n, slots[0, base + start + i]] = held[i]
                        return carry

                    lax.fori_loop(0, (hi - lo) // unroll, move, 0)
            spot = slots[0, length // PAGE]
            paged[n, spot] = patched(paged[n, spot])
            done = pltpu.make_async_copy(paged.at[n], pool.at[k, l, head], out_sems.at[n])
            done.start()
        flushes.append(done)

        if k == 0:
            query = queries[l, head]
            scale = 1.0 / math.sqrt(depth)
            for ref, e, lo, hi in parts:
                for f in range(fanout):
                    scores[f * sources + (mine ^ e), :, lo * PAGE : hi * PAGE] = lax.dot_general(
                        query,
                        ref[f].reshape((hi - lo) * PAGE, depth),
                        (((1,), (1,)), ((), ())),
                        preferred_element_type=jnp.float32,
                    )
            fresh_score = jnp.sum(query.astype(jnp.float32) * row, axis=-1, keepdims=True)
            values = jnp.where(places == length, fresh_score[None], scores[...]) * scale
            masked = jnp.where(places <= length, values, -1e30)
            highest = jnp.max(jnp.max(masked, axis=-1, keepdims=True), axis=0, keepdims=True)
            exponent = jnp.where(places <= length, jnp.exp(masked - highest), 0.0)
            total = jnp.sum(jnp.sum(exponent, axis=-1, keepdims=True), axis=0, keepdims=True)
            if l in probs_out:
                probs_out[l][...] = (exponent / total).astype(jnp.bfloat16)
                probs_now[l] = probs_out[l]
        else:
            weights = probs_now[l]
            weighted = sums[group, l][...] if (group, l) in sums else None
            if weighted is None:
                at_fresh = jnp.where(places == length, weights[...].astype(jnp.float32), 0.0)
                share = jnp.sum(jnp.sum(at_fresh, axis=-1, keepdims=True), axis=0)
                weighted = share * row
            for ref, e, lo, hi in parts:
                for f in range(fanout):
                    rank = f * sources + (mine ^ e)
                    mix = weights[rank, :, lo * PAGE : hi * PAGE].astype(jnp.float32)
                    at = lax.broadcasted_iota(jnp.int32, mix.shape, 1)
                    at += rank * blocks * PAGE + lo * PAGE
                    mix = jnp.where(at == length, 0.0, mix).astype(jnp.bfloat16)
                    weighted += jnp.dot(
                        mix,
                        ref[f].reshape((hi - lo) * PAGE, depth),
                        preferred_element_type=jnp.float32,
                    )
            sums[group, l] = weighted
            if l in sums_out:
                sums_out[l][...] = weighted
    if plan["final"]:
        for l in range(queries.shape[0]):
            for h in range(heads):
                mixed = jnp.zeros((per_head, depth), jnp.float32)
                for g in range(heads):
                    picked = (me // sources) ^ g == h
                    mixed = jnp.where(picked, sums[g, l][...], mixed)
                here = pl.ds(h * per_head, per_head)
                attention_out[l, here, :] = mixed.astype(attention_out.dtype)
    for flush in flushes:
        flush.wait()


def head_call(plan, args, operands, probs, sums, pool, pool_shape):
    slots, lengths, queries, fresh, spread = args
    fanout, blocks, _, depth = spread.shape[3:]
    layers, heads, per_head, _ = queries.shape
    units, group, sources = plan["units"], plan["group"], plan["sources"]
    ranks = fanout * sources
    plan = dict(plan, piece=spread.shape[3:], heads=heads, kv_heads=fresh.shape[3])
    plan["operands"] = len(operands)
    plan["has_pool"] = pool is not None
    value_layers = [l for k, l in units if k == 1]
    plan["probs_out"] = [l for k, l in units if k == 0]
    plan["given_probs"] = [l for l in value_layers if l not in plan["probs_out"]]
    if plan["final"]:
        plan["sums_in"], plan["sums_out"] = list(sums), []
    else:
        plan["sums_in"], plan["sums_out"] = [], value_layers
    smem = pl.BlockSpec(memory_space=pltpu.SMEM)
    vmem = pl.BlockSpec(memory_space=pltpu.VMEM)
    anywhere = pl.BlockSpec(memory_space=pl.ANY)
    inputs = [slots, lengths, queries, fresh] + ([spread] if plan["own"] else [])
    in_specs = [smem, smem, vmem, vmem] + (
        [pl.BlockSpec(memory_space=pltpu.HBM)] if plan["own"] else []
    )
    inside = [*operands, *(probs[group, l] for l in plan["given_probs"])]
    inside += [sums[name] for name in plan["sums_in"]]
    inputs += inside
    in_specs += [vmem] * len(inside)
    aliases = {}
    if pool is not None:
        aliases = {len(inputs): 0}
        inputs.append(pool)
        in_specs.append(anywhere)
    prob_shape = jax.ShapeDtypeStruct((ranks, per_head, blocks * PAGE), jnp.bfloat16)
    out_shape = [jax.ShapeDtypeStruct(pool_shape, jnp.bfloat16)]
    out_shape += [prob_shape] * len(plan["probs_out"])
    out_shape += [jax.ShapeDtypeStruct((per_head, depth), jnp.float32)] * len(plan["sums_out"])
    if plan["final"]:
        out_shape.append(jax.ShapeDtypeStruct((layers, heads * per_head, depth), jnp.bfloat16))
    count = len(units)
    own_shape = (count, *spread.shape[3:]) if plan["own"] else (1, 1, 1, PAGE, depth)
    results = list(pl.pallas_call(
        functools.partial(head_kernel, plan),
        out_shape=out_shape,
        in_specs=in_specs,
        out_specs=[anywhere] + [vmem] * (len(out_shape) - 1),
        scratch_shapes=[
            pltpu.VMEM((ranks, per_head, blocks * PAGE), jnp.float32),
            pltpu.VMEM((count, ranks * blocks, PAGE, depth), jnp.bfloat16),
            pltpu.VMEM(own_shape, jnp.bfloat16),
            pltpu.SemaphoreType.DMA((count,)),
            pltpu.SemaphoreType.DMA((count,)),
        ],
        input_output_aliases=aliases,
        compiler_params=pltpu.CompilerParams(vmem_limit_bytes=16 << 20),
        cost_estimate=pl.CostEstimate(
            flops=0, bytes_accessed=count * 4 * ranks * blocks * PAGE * depth * 2, transcendentals=0
        ),
    )(*inputs))
    pool = results.pop(0)
    for l in plan["probs_out"]:
        probs[group, l] = results.pop(0)
    for l in plan["sums_out"]:
        sums[group, l] = results.pop(0)
    return pool, results.pop(0) if plan["final"] else None


def body(tp_ranks, seq_ranks, kv_prefill, queries, new_kv, lengths, page_slots):
    return handoff(tp_ranks, seq_ranks, kv_prefill, queries, new_kv, lengths, page_slots)


def handoff(tp_ranks, seq_ranks, kv_prefill, queries, new_kv, lengths, page_slots):
    kv_heads = new_kv.shape[3]
    layers = kv_prefill.shape[1]
    depth = kv_prefill.shape[4]
    heads = max(1, kv_heads // tp_ranks)
    fanout = tp_ranks * heads // kv_heads
    sources = seq_ranks // heads
    blocks = kv_prefill.shape[3] // PAGE
    pages = page_slots.shape[1]

    spread = spread_heads(kv_prefill, fanout)
    spread = spread.reshape(2, layers, spread.shape[2], fanout, blocks, PAGE, depth)
    units = [(k, l) for k in (0, 1) for l in range(layers)]
    quarter = max(1, blocks // 4)
    far = range(sources, seq_ranks)

    sends = []
    for k, l in units:
        spans = [(0, blocks)]
        if (k, l) == units[0]:
            spans = [(0, quarter), (quarter, blocks)]
        elif (k, l) == units[-1]:
            spans = [(0, blocks - quarter), (blocks - quarter, blocks)]
        for lo, hi in spans:
            stage = 0 if (k, l) == units[0] and lo == 0 else 1
            sends += [(stage, delta, [(k, l, lo, hi)]) for delta in far]
    sends += [(2, delta, [(k, l, 0, blocks) for k, l in units]) for delta in range(1, sources)]
    arrived = []
    after = []
    for stage in range(3):
        batch = [(delta, items) for at, delta, items in sends if at == stage]
        if not batch:
            continue
        wanted = [[(k, l, delta, lo, hi) for k, l, lo, hi in items] for delta, items in batch]
        blocks_out = cut(spread, wanted, after)
        after = [blocks_out[0]]
        for (delta, items), block in zip(batch, blocks_out):
            arrived.append((delta, items, swapped(block, "seq", delta)))

    grouped = queries.reshape(layers, heads, queries.shape[2] // heads, depth)
    args = (page_slots, lengths, grouped, new_kv, spread)
    pool_shape = (2, layers, heads, pages, PAGE, depth)
    probs, sums = {}, {}

    def launch(units, group, chosen, pool, own=False, final=False, close=False):
        parts = [
            (at, row, (k, l), delta - group * sources, lo, hi)
            for at, (delta, items, _) in enumerate(chosen)
            for row, (k, l, lo, hi) in enumerate(items)
        ]
        plan = dict(
            units=units, group=group, sources=sources, parts=parts, own=own, final=final,
            close=close, tp_ranks=tp_ranks,
        )
        operands = [block for _, _, block in chosen]
        return head_call(plan, args, operands, probs, sums, pool, pool_shape)

    near = [a for a in arrived if a[0] < sources]
    pool, out = launch(units, 0, near, None, own=True, final=heads == 1)
    for group in range(1, heads):
        for unit in units:
            chosen = [a for a in arrived if a[0] // sources == group and a[1][0][:2] == unit]
            if unit == units[-1]:
                early = [a for a in chosen if a[1][0][2] == 0]
                pool, _ = launch([unit], group, early, pool)
                chosen = [a for a in chosen if a[1][0][2] > 0]
                pool, out = launch(
                    [unit], group, chosen, pool, final=group == heads - 1, close=True
                )
            else:
                pool, _ = launch([unit], group, chosen, pool)
    return pool, out.reshape(queries.shape)


def solution(mesh):
    placed = (
        P(None, None, "groups", ("tp", "seq"), None),
        P(None, ("groups", "seq"), "tp", None),
        P(None, None, ("groups", "seq"), None, None),
        P(("groups", "seq")),
        P(("groups", "seq"), None),
    )
    return jax.shard_map(
        functools.partial(body, mesh.shape["tp"], mesh.shape["seq"]),
        mesh=mesh,
        in_specs=placed,
        out_specs=(
            P(None, None, "tp", ("groups", "seq"), None, None),
            P(None, ("groups", "seq"), "tp", None),
        ),
        check_vma=False,
    )
```

time: 179 us -> 102 us (0.57)
  local copies, waits for them, and re-layouts: 60.9 us -> 3.41 us
  waiting for transfers between devices: 86.6 us -> 64 us
  Pallas kernels: 0 us -> 18.3 us
  other arithmetic: 14.9 us -> 0.01 us
  starting transfers between devices: 5.79 us -> 14.8 us
  matrix products: 7.1 us -> 0 us
  between operations: 3.37 us -> 1.46 us
    all_to_all x1 -> x0, waiting for transfers between devices: 86.6 us -> none  [body(): lax.all_to_all(shaped, 'seq', split_axis=2, concat_axis=4, tiled=True)]
    ppermute x0 -> x13, waiting for transfers between devices: none -> 64 us  [swapped(): lax.ppermute(array, axis, [(i, i ^ bits) for i in range(lax.axis_size(axi...]
    gather x3 -> x0, local copies, waits for them, and re-layouts: 23 us -> none  [the longest x1 12.5 us: repack(): return jnp.take(paged_rows, inverse, axis=3)]
    pallas_call x0 -> x9, Pallas kernels: none -> 18.3 us  [the longest x6 16.5 us: head_call(): pl.pallas_call(functools.partial(head_kernel, plan), out_shape=out_shape,...]
    ppermute x0 -> x13, starting transfers between devices: none -> 14.8 us  [swapped(): lax.ppermute(array, axis, [(i, i ^ bits) for i in range(lax.axis_size(axi...]
    unnamed x6 -> x12, local copies, waits for them, and re-layouts: 15.9 us -> 3.41 us
    select_n x3 -> x0, other arithmetic: 11.7 us -> none  [the longest x2 7.44 us: repack(): return jnp.take(paged_rows, inverse, axis=3)]
    all_to_all x1 -> x0, local copies, waits for them, and re-layouts: 7.59 us -> none  [body(): lax.all_to_all(shaped, 'seq', split_axis=2, concat_axis=4, tiled=True)]
  transfers between devices with their start and end apart: 1 -> 13, of which waited for: 1 -> 11; matrix products, arithmetic and copies ran while one was open for 3% -> 0% of each run, Pallas kernels for 0% -> 14%
where the time goes in v1:
time: 102 us
  waiting for transfers between devices  64 us (63%)
  Pallas kernels  18.3 us (18%)
  starting transfers between devices  14.8 us (15%)
  local copies, waits for them, and re-layouts  3.41 us (3%)
  between operations  1.46 us (1%)
    ppermute x13, waiting for transfers between devices, swapped(): lax.ppermute(array, axis, [(i, i ^ bits) for i in range(lax.axis_size(axi...  64 us
    pallas_call x6, Pallas kernels, head_call(): pl.pallas_call(functools.partial(head_kernel, plan), out_shape=out_shape,...  16.5 us
    ppermute x13, starting transfers between devices, swapped(): lax.ppermute(array, axis, [(i, i ^ bits) for i in range(lax.axis_size(axi...  14.8 us
    unnamed x12, local copies, waits for them, and re-layouts  3.41 us
  transfers between devices with their start and end apart: 13, of which 11 were waited for; matrix products, arithmetic and copies ran while one was open for 0% of the time, Pallas kernels for 14%

profile of v1, /device:TPU:0, one launch (start us, length us, event | category | flops | bytes accessed | tf_op | source)
XLA Modules:
  0.0 102.0 jit_solution(922457313879642161)
XLA Ops:
  0.6 3.4 %copy-done = bf16[2,2,4,2048,128]{4,3,2,1,0:T(8,128)(2,1)S(1)} copy-done((bf16[2,2,4,2048,128]{4,3,2,1,0:T(8,128)(2,1)S(1)}, bf16[2,2,4,2048,128]{4,3,2,1,0:T(8,128)(2,1)}, u32[]{:S(2)}) %copy-start) | copy-done | bytes 8388632
  4.0 0.3 shard_map.68
  4.4 1.3 %shard_map.69 = (bf16[1,1,96,16,128]{4,3,2,1,0:T(8,128)(2,1)S(1)}, bf16[1,1,96,16,128]{4,3,2,1,0:T(8,128)(2,1)S(1)}, bf16[1,1,128,16,128]{4,3,2,1,0:T(8,128)(2,1...) custom-call(bf16[2,2,4,1,128,16,128]{6,5,4,3,2,1,0:T(8,128)(2,1)S(1), ...), custom_call_target="tpu_custom_call" | custom-call | bytes 7864320 | tf_op jit(solution)/shard_map/pallas_call | solution.py:50
  5.8 0.2 shard_map.70
  6.0 0.6 collective-permute-start.8
  6.5 2.6 %collective-permute-start.5 = (bf16[1,1,32,16,128]{4,3,2,1,0:T(8,128)(2,1)S(1)}, bf16[1,1,32,16,128]{4,3,2,1,0:T(8,128)(2,1)S(1)}, u32[]{:S(2)}, u32[]{:S(2)}) collective-permute-start(bf16[1,1,32,16,128]{4,3,2,1,0:T(8,128)(2,1)S(1)} %get-tuple-element.32), channel_id=1, source_target_pairs={{0,3},{1,2},{2,1},{3,0},{4,7},{5,6},{6,5},{7,4},{8,11},{9,10},{10,... | collective-permute-start | bytes 393224 | tf_op jit(solution)/shard_map/ppermute | solution.py:17
  9.2 1.4 %collective-permute-start.7 = (bf16[1,1,96,16,128]{4,3,2,1,0:T(8,128)(2,1)S(1)}, bf16[1,1,96,16,128]{4,3,2,1,0:T(8,128)(2,1)S(1)}, u32[]{:S(2)}, u32[]{:S(2)}) collective-permute-start(bf16[1,1,96,16,128]{4,3,2,1,0:T(8,128)(2,1)S(1)} %get-tuple-element.34), channel_id=1, source_target_pairs={{0,3},{1,2},{2,1},{3,0},{4,7},{5,6},{6,5},{7,4},{8,11},{9,10},{10,... | collective-permute-start | bytes 1179656 | tf_op jit(solution)/shard_map/ppermute | solution.py:17
  10.5 0.6 collective-permute-start.6
  11.1 1.9 %collective-permute-done.5.refs_5_ = bf16[1,1,32,16,128]{4,3,2,1,0:T(8,128)(2,1)S(1)} collective-permute-done((bf16[1,1,32,16,128]{4,3,2,1,0:T(8,128)(2,1)S(1)}, bf16[1,1,32,16,128]{4,3,2,1,0:T(8,128)(2,1)S(1)}, u32[]{:S(2)}, u32[]{:S(2)}) %collective-permute-start.5) | collective-permute-done | bytes 131104 | tf_op jit(solution)/shard_map/ppermute | solution.py:17
  13.0 1.3 %collective-permute-start.2 = (bf16[1,1,128,16,128]{4,3,2,1,0:T(8,128)(2,1)S(1)}, bf16[1,1,128,16,128]{4,3,2,1,0:T(8,128)(2,1)S(1)}, u32[]{:S(2)}, u32[]{:S(2)}) collective-permute-start(bf16[1,1,128,16,128]{4,3,2,1,0:T(8,128)(2,1)S(1)} %get-tuple-element.30), channel_id=1, source_target_pairs={{0,2},{1,3},{2,0},{3,1},{4,6},{5,7},{6,4},{7,5},{8,10},{9,11},{10,... | collective-permute-start | bytes 1572872 | tf_op jit(solution)/shard_map/ppermute | solution.py:17
  14.3 2.0 %collective-permute-done.4.refs_4_ = bf16[1,1,32,16,128]{4,3,2,1,0:T(8,128)(2,1)S(1)} collective-permute-done((bf16[1,1,32,16,128]{4,3,2,1,0:T(8,128)(2,1)S(1)}, bf16[1,1,32,16,128]{4,3,2,1,0:T(8,128)(2,1)S(1)}, u32[]{:S(2)}, u32[]{:S(2)}) %collective-permute-start.4) | collective-permute-done | bytes 131104 | tf_op jit(solution)/shard_map/ppermute | solution.py:17
  16.2 0.6 collective-permute-start.3
  16.8 7.4 %collective-permute-done.7.refs_7_ = bf16[1,1,96,16,128]{4,3,2,1,0:T(8,128)(2,1)S(1)} collective-permute-done((bf16[1,1,96,16,128]{4,3,2,1,0:T(8,128)(2,1)S(1)}, bf16[1,1,96,16,128]{4,3,2,1,0:T(8,128)(2,1)S(1)}, u32[]{:S(2)}, u32[]{:S(2)}) %collective-permute-start.7) | collective-permute-done | bytes 393248 | tf_op jit(solution)/shard_map/ppermute | solution.py:17
  24.2 1.3 %collective-permute-start.9 = (bf16[1,1,128,16,128]{4,3,2,1,0:T(8,128)(2,1)S(1)}, bf16[1,1,128,16,128]{4,3,2,1,0:T(8,128)(2,1)S(1)}, u32[]{:S(2)}, u32[]{:S(2)}) collective-permute-start(bf16[1,1,128,16,128]{4,3,2,1,0:T(8,128)(2,1)S(1)} %get-tuple-element.40), channel_id=1, source_target_pairs={{0,2},{1,3},{2,0},{3,1},{4,6},{5,7},{6,4},{7,5},{8,10},{9,11},{10,... | collective-permute-start | bytes 1572872 | tf_op jit(solution)/shard_map/ppermute | solution.py:17
  25.5 7.6 %collective-permute-done.6.refs_6_ = bf16[1,1,96,16,128]{4,3,2,1,0:T(8,128)(2,1)S(1)} collective-permute-done((bf16[1,1,96,16,128]{4,3,2,1,0:T(8,128)(2,1)S(1)}, bf16[1,1,96,16,128]{4,3,2,1,0:T(8,128)(2,1)S(1)}, u32[]{:S(2)}, u32[]{:S(2)}) %collective-permute-start.6) | collective-permute-done | bytes 393248 | tf_op jit(solution)/shard_map/ppermute | solution.py:17
  33.1 0.6 collective-permute-start.10
  33.6 10.7 %collective-permute-done.2.refs_4_ = bf16[1,1,128,16,128]{4,3,2,1,0:T(8,128)(2,1)S(1)} collective-permute-done((bf16[1,1,128,16,128]{4,3,2,1,0:T(8,128)(2,1)S(1)}, bf16[1,1,128,16,128]{4,3,2,1,0:T(8,128)(2,1)S(1)}, u32[]{:S(2)}, u32[]{:S(2)}) %collective-permute-start.2) | collective-permute-done | bytes 524320 | tf_op jit(solution)/shard_map/ppermute | solution.py:17
  44.3 2.1 %collective-permute-start.11 = (bf16[1,1,96,16,128]{4,3,2,1,0:T(8,128)(2,1)S(1)}, bf16[1,1,96,16,128]{4,3,2,1,0:T(8,128)(2,1)S(1)}, u32[]{:S(2)}, u32[]{:S(2)}) collective-permute-start(bf16[1,1,96,16,128]{4,3,2,1,0:T(8,128)(2,1)S(1)} %get-tuple-element.45), channel_id=1, source_target_pairs={{0,2},{1,3},{2,0},{3,1},{4,6},{5,7},{6,4},{7,5},{8,10},{9,11},{10,... | collective-permute-start | bytes 1179656 | tf_op jit(solution)/shard_map/ppermute | solution.py:17
  46.4 8.8 %collective-permute-done.3.refs_5_ = bf16[1,1,128,16,128]{4,3,2,1,0:T(8,128)(2,1)S(1)} collective-permute-done((bf16[1,1,128,16,128]{4,3,2,1,0:T(8,128)(2,1)S(1)}, bf16[1,1,128,16,128]{4,3,2,1,0:T(8,128)(2,1)S(1)}, u32[]{:S(2)}, u32[]{:S(2)}) %collective-permute-start.3) | collective-permute-done | bytes 524320 | tf_op jit(solution)/shard_map/ppermute | solution.py:17
  55.1 1.9 %collective-permute-start.12 = (bf16[1,1,96,16,128]{4,3,2,1,0:T(8,128)(2,1)S(1)}, bf16[1,1,96,16,128]{4,3,2,1,0:T(8,128)(2,1)S(1)}, u32[]{:S(2)}, u32[]{:S(2)}) collective-permute-start(bf16[1,1,96,16,128]{4,3,2,1,0:T(8,128)(2,1)S(1)} %get-tuple-element.46), channel_id=1, source_target_pairs={{0,3},{1,2},{2,1},{3,0},{4,7},{5,6},{6,5},{7,4},{8,11},{9,10},{10,... | collective-permute-start | bytes 1179656 | tf_op jit(solution)/shard_map/ppermute | solution.py:17
  57.0 9.8 %collective-permute-done.9.refs_4_ = bf16[1,1,128,16,128]{4,3,2,1,0:T(8,128)(2,1)S(1)} collective-permute-done((bf16[1,1,128,16,128]{4,3,2,1,0:T(8,128)(2,1)S(1)}, bf16[1,1,128,16,128]{4,3,2,1,0:T(8,128)(2,1)S(1)}, u32[]{:S(2)}, u32[]{:S(2)}) %collective-permute-start.9) | collective-permute-done | bytes 524320 | tf_op jit(solution)/shard_map/ppermute | solution.py:17
  66.8 2.1 %collective-permute-start = (bf16[1,1,32,16,128]{4,3,2,1,0:T(8,128)(2,1)S(1)}, bf16[1,1,32,16,128]{4,3,2,1,0:T(8,128)(2,1)S(1)}, u32[]{:S(2)}, u32[]{:S(2)}) collective-permute-start(bf16[1,1,32,16,128]{4,3,2,1,0:T(8,128)(2,1)S(1)} %get-tuple-element.28), channel_id=1, source_target_pairs={{0,2},{1,3},{2,0},{3,1},{4,6},{5,7},{6,4},{7,5},{8,10},{9,11},{10,... | collective-permute-start | bytes 393224 | tf_op jit(solution)/shard_map/ppermute | solution.py:17
  69.6 5.6 %shard_map.71 = (bf16[2,2,2,256,16,128]{5,4,3,2,1,0:T(8,128)(2,1)}, bf16[2,8,2048]{2,1,0:T(8,128)(2,1)}, bf16[2,8,2048]{2,1,0:T(8,128)(2,1)}, f32[8,128]{1,0:T(8,128)S(1)}, f32[8,128]{1,0:T(8,128)S(1)}) custom-call(s32[1,256]{1,0:T(1,128)S(1)} %copy-done.3, s32[1]{0:T(128)S(6)} %copy.18.refs_1_, bf16[2,2,8,128]{3,2,1,0:T(8,128)(2,1)S(1)} %bitcast.11, ...), custom_call_target="tpu_custom_call" | custom-call | bytes 16777216 | tf_op jit(solution)/shard_map/pallas_call | solution.py:260
  75.1 2.5 %shard_map.72 = (bf16[2,2,2,256,16,128]{5,4,3,2,1,0:T(8,128)(2,1)}, bf16[2,8,2048]{2,1,0:T(8,128)(2,1)S(1)}) custom-call(s32[1,256]{1,0:T(1,128)S(1)} %copy-done.3, s32[1]{0:T(128)S(6)} %copy.18.refs_1_, bf16[2,2,8,128]{3,2,1,0:T(8,128)(2,1)S(1)} %bitcast.12, bf16[2,2,1,8,128]{4,3,2,1,0:T(8,128)(2,1)S(1)} %copy-done.2, ...), custom_call_target="tpu_custom_call", output_to_operand_aliasing={{0}: (8, {})} | custom-call | bytes 4194304 | tf_op jit(solution)/shard_map/pallas_call | solution.py:260
  77.6 2.5 %shard_map.73 = (bf16[2,2,2,256,16,128]{5,4,3,2,1,0:T(8,128)(2,1)}, bf16[2,8,2048]{2,1,0:T(8,128)(2,1)S(1)}) custom-call(s32[1,256]{1,0:T(1,128)S(1)} %copy-done.3, s32[1]{0:T(128)S(6)} %copy.18.refs_1_, bf16[2,2,8,128]{3,2,1,0:T(8,128)(2,1)S(1)} %bitcast.13, bf16[2,2,1,8,128]{4,3,2,1,0:T(8,128)(2,1)S(1)} %copy-done.2, ...), custom_call_target="tpu_custom_call", output_to_operand_aliasing={{0}: (6, {})} | custom-call | bytes 4194304 | tf_op jit(solution)/shard_map/pallas_call | solution.py:260
  80.1 2.1 %shard_map.74 = (bf16[2,2,2,256,16,128]{5,4,3,2,1,0:T(8,128)(2,1)}, f32[8,128]{1,0:T(8,128)S(1)}) custom-call(s32[1,256]{1,0:T(1,128)S(1)} %copy-done.3, s32[1]{0:T(128)S(6)} %copy.18.refs_1_, bf16[2,2,8,128]{3,2,1,0:T(8,128)(2,1)S(1)} %bitcast.14, bf16[2,2,1,8,128]{4,3,2,1,0:T(8,128)(2,1)S(1)} %copy-done.2, ...), custom_call_target="tpu_custom_call", output_to_operand_aliasing={{0}: (7, {})} | custom-call | bytes 4194304 | tf_op jit(solution)/shard_map/pallas_call | solution.py:260
  82.1 4.3 %collective-permute-done.11.refs_4_ = bf16[1,1,96,16,128]{4,3,2,1,0:T(8,128)(2,1)S(1)} collective-permute-done((bf16[1,1,96,16,128]{4,3,2,1,0:T(8,128)(2,1)S(1)}, bf16[1,1,96,16,128]{4,3,2,1,0:T(8,128)(2,1)S(1)}, u32[]{:S(2)}, u32[]{:S(2)}) %collective-permute-start.11) | collective-permute-done | bytes 393248 | tf_op jit(solution)/shard_map/ppermute | solution.py:17
  86.5 8.0 %collective-permute-done.12.refs_5_ = bf16[1,1,96,16,128]{4,3,2,1,0:T(8,128)(2,1)S(1)} collective-permute-done((bf16[1,1,96,16,128]{4,3,2,1,0:T(8,128)(2,1)S(1)}, bf16[1,1,96,16,128]{4,3,2,1,0:T(8,128)(2,1)S(1)}, u32[]{:S(2)}, u32[]{:S(2)}) %collective-permute-start.12) | collective-permute-done | bytes 393248 | tf_op jit(solution)/shard_map/ppermute | solution.py:17
  94.5 1.9 %shard_map.75 = (bf16[2,2,2,256,16,128]{5,4,3,2,1,0:T(8,128)(2,1)}, f32[8,128]{1,0:T(8,128)S(1)}) custom-call(s32[1,256]{1,0:T(1,128)S(1)} %copy-done.3, s32[1]{0:T(128)S(6)} %copy.18.refs_1_, bf16[2,2,8,128]{3,2,1,0:T(8,128)(2,1)S(1)} %bitcast.15, bf16[2,2,1,8,128]{4,3,2,1,0:T(8,128)(2,1)S(1)} %copy-done.2, ...), custom_call_target="tpu_custom_call", output_to_operand_aliasing={{0}: (7, {})} | custom-call | bytes 4194304 | tf_op jit(solution)/shard_map/pallas_call | solution.py:260
  96.4 1.3 %collective-permute-done.refs_4_ = bf16[1,1,32,16,128]{4,3,2,1,0:T(8,128)(2,1)S(1)} collective-permute-done((bf16[1,1,32,16,128]{4,3,2,1,0:T(8,128)(2,1)S(1)}, bf16[1,1,32,16,128]{4,3,2,1,0:T(8,128)(2,1)S(1)}, u32[]{:S(2)}, u32[]{:S(2)}) %collective-permute-start) | collective-permute-done | bytes 131104 | tf_op jit(solution)/shard_map/ppermute | solution.py:17
  97.7 2.3 %collective-permute-done.1.refs_5_ = bf16[1,1,32,16,128]{4,3,2,1,0:T(8,128)(2,1)S(1)} collective-permute-done((bf16[1,1,32,16,128]{4,3,2,1,0:T(8,128)(2,1)S(1)}, bf16[1,1,32,16,128]{4,3,2,1,0:T(8,128)(2,1)S(1)}, u32[]{:S(2)}, u32[]{:S(2)}) %collective-permute-start.1) | collective-permute-done | bytes 131104 | tf_op jit(solution)/shard_map/ppermute | solution.py:17
  100.0 2.0 %shard_map.76 = (bf16[2,2,2,256,16,128]{5,4,3,2,1,0:T(8,128)(2,1)}, bf16[2,16,128]{2,1,0:T(8,128)(2,1)}) custom-call(s32[1,256]{1,0:T(1,128)S(1)} %copy-done.3, s32[1]{0:T(128)S(6)} %copy.18.refs_1_, bf16[2,2,8,128]{3,2,1,0:T(8,128)(2,1)S(1)} %bitcast.16, bf16[2,2,1,8,128]{4,3,2,1,0:T(8,128)(2,1)S(1)} %copy-done.2, ...), custom_call_target="tpu_custom_call", output_to_operand_aliasing={{0}: (11, {})} | custom-call | bytes 4194304 | tf_op jit(solution)/shard_map/pallas_call | solution.py:260
  (16 shorter events, 0.1 us)
Async XLA Ops:
  0.6 3.4 %copy-start = (bf16[2,2,4,2048,128]{4,3,2,1,0:T(8,128)(2,1)S(1)}, bf16[2,2,4,2048,128]{4,3,2,1,0:T(8,128)(2,1)}, u32[]{:S(2)}) copy-start(bf16[2,2,4,2048,128]{4,3,2,1,0:T(8,128)(2,1)} %param.5) | copy-start | bytes 25165828
  4.3 65.2 %slice-start = ((s8[8388608]{0:T(1024)(128)(4,1)}), s8[4194304]{0:T(1024)(128)(4,1)S(1)}, s32[]{:S(2)}) async-start(s8[8388608]{0:T(1024)(128)(4,1)} %bitcast.8), calls=%async_computation | async-start | bytes 8388608
  4.4 65.2 %copy-start.1 = (bf16[2,1,16,128]{3,2,1,0:T(8,128)(2,1)S(1)}, bf16[2,1,16,128]{3,2,1,0:T(8,128)(2,1)}, u32[]{:S(2)}) copy-start(bf16[2,1,16,128]{3,2,1,0:T(8,128)(2,1)} %param.6) | copy-start | bytes 24580
  4.4 65.2 %copy-start.2 = (bf16[2,2,1,8,128]{4,3,2,1,0:T(8,128)(2,1)S(1)}, bf16[2,2,1,8,128]{4,3,2,1,0:T(8,128)(2,1)}, u32[]{:S(2)}) copy-start(bf16[2,2,1,8,128]{4,3,2,1,0:T(8,128)(2,1)} %refs_3_.11) | copy-start | bytes 24580
  4.4 65.2 %copy-start.3 = (s32[1,256]{1,0:T(1,128)S(1)}, s32[1,256]{1,0:T(1,128)}, u32[]{:S(2)}) copy-start(s32[1,256]{1,0:T(1,128)} %refs_0_.11) | copy-start | bytes 3076
  5.7 63.8 %slice-start.1 = ((s8[8388608]{0:T(1024)(128)(4,1)}), s8[4194304]{0:T(1024)(128)(4,1)S(1)}, s32[]{:S(2)}) async-start(s8[8388608]{0:T(1024)(128)(4,1)} %bitcast.8), calls=%async_computation.1 | async-start | bytes 8388608
  6.0 62.9 %collective-permute-start.8 = (bf16[4,1,128,16,128]{4,3,2,1,0:T(8,128)(2,1)S(1)}, bf16[4,1,128,16,128]{4,3,2,1,0:T(8,128)(2,1)S(1)}, u32[]{:S(2)}, u32[]{:S(2)}) collective-permute-start(bf16[4,1,128,16,128]{4,3,2,1,0:T(8,128)(2,1)S(1)} %shard_map.70), channel_id=1, source_target_pairs={{0,1},{1,0},{2,3},{3,2},{4,5},{5,4},{6,7},{7,6},{8,9},{9,8},{10,11... | collective-permute-start | bytes 6291464 | tf_op jit(solution)/shard_map/ppermute | solution.py:17
  6.5 6.5 %collective-permute-start.5 = (bf16[1,1,32,16,128]{4,3,2,1,0:T(8,128)(2,1)S(1)}, bf16[1,1,32,16,128]{4,3,2,1,0:T(8,128)(2,1)S(1)}, u32[]{:S(2)}, u32[]{:S(2)}) collective-permute-start(bf16[1,1,32,16,128]{4,3,2,1,0:T(8,128)(2,1)S(1)} %get-tuple-element.32), channel_id=1, source_target_pairs={{0,3},{1,2},{2,1},{3,0},{4,7},{5,6},{6,5},{7,4},{8,11},{9,10},{10,... | collective-permute-start | bytes 393224 | tf_op jit(solution)/shard_map/ppermute | solution.py:17
  9.1 7.1 %collective-permute-start.4 = (bf16[1,1,32,16,128]{4,3,2,1,0:T(8,128)(2,1)S(1)}, bf16[1,1,32,16,128]{4,3,2,1,0:T(8,128)(2,1)S(1)}, u32[]{:S(2)}, u32[]{:S(2)}) collective-permute-start(bf16[1,1,32,16,128]{4,3,2,1,0:T(8,128)(2,1)S(1)} %get-tuple-element.27.refs_1_), channel_id=1, source_target_pairs={{0,2},{1,3},{2,0},{3,1},{4,6},{5,7},{6,4},{7,5},{8,10},{9,11},{10,... | collective-permute-start | bytes 393224 | tf_op jit(solution)/shard_map/ppermute | solution.py:17
  9.2 15.1 %collective-permute-start.7 = (bf16[1,1,96,16,128]{4,3,2,1,0:T(8,128)(2,1)S(1)}, bf16[1,1,96,16,128]{4,3,2,1,0:T(8,128)(2,1)S(1)}, u32[]{:S(2)}, u32[]{:S(2)}) collective-permute-start(bf16[1,1,96,16,128]{4,3,2,1,0:T(8,128)(2,1)S(1)} %get-tuple-element.34), channel_id=1, source_target_pairs={{0,3},{1,2},{2,1},{3,0},{4,7},{5,6},{6,5},{7,4},{8,11},{9,10},{10,... | collective-permute-start | bytes 1179656 | tf_op jit(solution)/shard_map/ppermute | solution.py:17
  10.5 22.5 %collective-permute-start.6 = (bf16[1,1,96,16,128]{4,3,2,1,0:T(8,128)(2,1)S(1)}, bf16[1,1,96,16,128]{4,3,2,1,0:T(8,128)(2,1)S(1)}, u32[]{:S(2)}, u32[]{:S(2)}) collective-permute-start(bf16[1,1,96,16,128]{4,3,2,1,0:T(8,128)(2,1)S(1)} %get-tuple-element.33.refs_1_), channel_id=1, source_target_pairs={{0,2},{1,3},{2,0},{3,1},{4,6},{5,7},{6,4},{7,5},{8,10},{9,11},{10,... | collective-permute-start | bytes 1179656 | tf_op jit(solution)/shard_map/ppermute | solution.py:17
  13.0 31.3 %collective-permute-start.2 = (bf16[1,1,128,16,128]{4,3,2,1,0:T(8,128)(2,1)S(1)}, bf16[1,1,128,16,128]{4,3,2,1,0:T(8,128)(2,1)S(1)}, u32[]{:S(2)}, u32[]{:S(2)}) collective-permute-start(bf16[1,1,128,16,128]{4,3,2,1,0:T(8,128)(2,1)S(1)} %get-tuple-element.30), channel_id=1, source_target_pairs={{0,2},{1,3},{2,0},{3,1},{4,6},{5,7},{6,4},{7,5},{8,10},{9,11},{10,... | collective-permute-start | bytes 1572872 | tf_op jit(solution)/shard_map/ppermute | solution.py:17
  16.2 38.9 %collective-permute-start.3 = (bf16[1,1,128,16,128]{4,3,2,1,0:T(8,128)(2,1)S(1)}, bf16[1,1,128,16,128]{4,3,2,1,0:T(8,128)(2,1)S(1)}, u32[]{:S(2)}, u32[]{:S(2)}) collective-permute-start(bf16[1,1,128,16,128]{4,3,2,1,0:T(8,128)(2,1)S(1)} %get-tuple-element.31), channel_id=1, source_target_pairs={{0,3},{1,2},{2,1},{3,0},{4,7},{5,6},{6,5},{7,4},{8,11},{9,10},{10,... | collective-permute-start | bytes 1572872 | tf_op jit(solution)/shard_map/ppermute | solution.py:17
  24.2 42.6 %collective-permute-start.9 = (bf16[1,1,128,16,128]{4,3,2,1,0:T(8,128)(2,1)S(1)}, bf16[1,1,128,16,128]{4,3,2,1,0:T(8,128)(2,1)S(1)}, u32[]{:S(2)}, u32[]{:S(2)}) collective-permute-start(bf16[1,1,128,16,128]{4,3,2,1,0:T(8,128)(2,1)S(1)} %get-tuple-element.40), channel_id=1, source_target_pairs={{0,2},{1,3},{2,0},{3,1},{4,6},{5,7},{6,4},{7,5},{8,10},{9,11},{10,... | collective-permute-start | bytes 1572872 | tf_op jit(solution)/shard_map/ppermute | solution.py:17
  33.1 47.0 %collective-permute-start.10 = (bf16[1,1,128,16,128]{4,3,2,1,0:T(8,128)(2,1)S(1)}, bf16[1,1,128,16,128]{4,3,2,1,0:T(8,128)(2,1)S(1)}, u32[]{:S(2)}, u32[]{:S(2)}) collective-permute-start(bf16[1,1,128,16,128]{4,3,2,1,0:T(8,128)(2,1)S(1)} %get-tuple-element.41), channel_id=1, source_target_pairs={{0,3},{1,2},{2,1},{3,0},{4,7},{5,6},{6,5},{7,4},{8,11},{9,10},{10,... | collective-permute-start | bytes 1572872 | tf_op jit(solution)/shard_map/ppermute | solution.py:17
  44.3 42.1 %collective-permute-start.11 = (bf16[1,1,96,16,128]{4,3,2,1,0:T(8,128)(2,1)S(1)}, bf16[1,1,96,16,128]{4,3,2,1,0:T(8,128)(2,1)S(1)}, u32[]{:S(2)}, u32[]{:S(2)}) collective-permute-start(bf16[1,1,96,16,128]{4,3,2,1,0:T(8,128)(2,1)S(1)} %get-tuple-element.45), channel_id=1, source_target_pairs={{0,2},{1,3},{2,0},{3,1},{4,6},{5,7},{6,4},{7,5},{8,10},{9,11},{10,... | collective-permute-start | bytes 1179656 | tf_op jit(solution)/shard_map/ppermute | solution.py:17
  55.1 39.3 %collective-permute-start.12 = (bf16[1,1,96,16,128]{4,3,2,1,0:T(8,128)(2,1)S(1)}, bf16[1,1,96,16,128]{4,3,2,1,0:T(8,128)(2,1)S(1)}, u32[]{:S(2)}, u32[]{:S(2)}) collective-permute-start(bf16[1,1,96,16,128]{4,3,2,1,0:T(8,128)(2,1)S(1)} %get-tuple-element.46), channel_id=1, source_target_pairs={{0,3},{1,2},{2,1},{3,0},{4,7},{5,6},{6,5},{7,4},{8,11},{9,10},{10,... | collective-permute-start | bytes 1179656 | tf_op jit(solution)/shard_map/ppermute | solution.py:17
  66.8 30.9 %collective-permute-start = (bf16[1,1,32,16,128]{4,3,2,1,0:T(8,128)(2,1)S(1)}, bf16[1,1,32,16,128]{4,3,2,1,0:T(8,128)(2,1)S(1)}, u32[]{:S(2)}, u32[]{:S(2)}) collective-permute-start(bf16[1,1,32,16,128]{4,3,2,1,0:T(8,128)(2,1)S(1)} %get-tuple-element.28), channel_id=1, source_target_pairs={{0,2},{1,3},{2,0},{3,1},{4,6},{5,7},{6,4},{7,5},{8,10},{9,11},{10,... | collective-permute-start | bytes 393224 | tf_op jit(solution)/shard_map/ppermute | solution.py:17
  68.9 31.1 %collective-permute-start.1 = (bf16[1,1,32,16,128]{4,3,2,1,0:T(8,128)(2,1)S(1)}, bf16[1,1,32,16,128]{4,3,2,1,0:T(8,128)(2,1)S(1)}, u32[]{:S(2)}, u32[]{:S(2)}) collective-permute-start(bf16[1,1,32,16,128]{4,3,2,1,0:T(8,128)(2,1)S(1)} %get-tuple-element.29), channel_id=1, source_target_pairs={{0,3},{1,2},{2,1},{3,0},{4,7},{5,6},{6,5},{7,4},{8,11},{9,10},{10,... | collective-permute-start | bytes 393224 | tf_op jit(solution)/shard_map/ppermute | solution.py:17

commit v2 on v1

--- a/solution.py
+++ b/solution.py
@@ -11,6 +11,7 @@
 
 PAGE = 16
 UNROLL = 16
+VMEM = 67_043_328
 
 
 def swapped(array, axis, bits):
@@ -40,7 +41,7 @@
         copy.wait()
 
 
-def cut(spread, wanted, after):
+def cut(spread, wanted, after, room):
     fanout, _, page, depth = spread.shape[3:]
     shapes = [
         jax.ShapeDtypeStruct((len(w), fanout, w[0][4] - w[0][3], page, depth), spread.dtype)
@@ -53,7 +54,7 @@
         in_specs=[pl.BlockSpec(memory_space=pltpu.HBM)] + [anywhere] * len(after),
         out_specs=[pl.BlockSpec(memory_space=pltpu.VMEM)] * len(shapes),
         scratch_shapes=[pltpu.SemaphoreType.DMA((sum(len(w) for w in wanted),))],
-        compiler_params=pltpu.CompilerParams(vmem_limit_bytes=8 << 20),
+        compiler_params=pltpu.CompilerParams(vmem_limit_bytes=VMEM - room),
         cost_estimate=pl.CostEstimate(
             flops=0, bytes_accessed=2 * sum(2 * math.prod(o.shape) for o in shapes), transcendentals=0
         ),
@@ -68,7 +69,6 @@
 
     units, group, sources = plan["units"], plan["group"], plan["sources"]
     slots, lengths, queries, fresh = take(4)
-    own_ref = take(1)[0] if plan["own"] else None
     operands = take(plan["operands"])
     given_probs = dict(zip(plan["given_probs"], take(len(plan["given_probs"]))))
     sums_in = dict(zip(plan["sums_in"], take(len(plan["sums_in"]))))
@@ -78,7 +78,7 @@
     probs_out = dict(zip(plan["probs_out"], take(len(plan["probs_out"]))))
     sums_out = dict(zip(plan["sums_out"], take(len(plan["sums_out"]))))
     attention_out = take(1)[0] if plan["final"] else None
-    scores, paged, own_buf, in_sems, out_sems = refs
+    scores, paged, mixed_buf, mixed_sem, out_sems = refs
 
     me = lax.axis_index("seq")
     mine = me % sources
@@ -90,23 +90,11 @@
     per_head = queries.shape[2]
     places = lax.broadcasted_iota(jnp.int32, scores.shape, 0) * (blocks * PAGE)
     places += lax.broadcasted_iota(jnp.int32, scores.shape, 2)
-    fetches = []
-    if plan["own"]:
-        for n, (k, l) in enumerate(units):
-            fetches.append(
-                pltpu.make_async_copy(own_ref.at[k, l, me], own_buf.at[n], in_sems.at[n])
-            )
-            fetches[-1].start()
-
     probs_now = dict(given_probs)
     sums = dict(sums_in)
     flushes = []
     for n, (k, l) in enumerate(units):
-        parts = []
-        if plan["own"]:
-            fetches[n].wait()
-            parts.append((own_buf.at[n], 0, 0, blocks))
-        parts += [
+        parts = [
             (operands[at].at[row], e, lo, hi)
             for at, row, unit, e, lo, hi in plan["parts"]
             if unit == (k, l)
@@ -212,18 +200,20 @@
                     picked = (me // sources) ^ g == h
                     mixed = jnp.where(picked, sums[g, l][...], mixed)
                 here = pl.ds(h * per_head, per_head)
-                attention_out[l, here, :] = mixed.astype(attention_out.dtype)
+                mixed_buf[l, here, :] = mixed.astype(mixed_buf.dtype)
+        flushes.append(pltpu.make_async_copy(mixed_buf, attention_out, mixed_sem))
+        flushes[-1].start()
     for flush in flushes:
         flush.wait()
 
 
 def head_call(plan, args, operands, probs, sums, pool, pool_shape):
-    slots, lengths, queries, fresh, spread = args
-    fanout, blocks, _, depth = spread.shape[3:]
+    slots, lengths, queries, fresh = args
+    fanout, blocks, _, depth = plan["piece"]
     layers, heads, per_head, _ = queries.shape
     units, group, sources = plan["units"], plan["group"], plan["sources"]
     ranks = fanout * sources
-    plan = dict(plan, piece=spread.shape[3:], heads=heads, kv_heads=fresh.shape[3])
+    plan = dict(plan, heads=heads, kv_heads=fresh.shape[3])
     plan["operands"] = len(operands)
     plan["has_pool"] = pool is not None
     value_layers = [l for k, l in units if k == 1]
@@ -236,10 +226,8 @@
     smem = pl.BlockSpec(memory_space=pltpu.SMEM)
     vmem = pl.BlockSpec(memory_space=pltpu.VMEM)
     anywhere = pl.BlockSpec(memory_space=pl.ANY)
-    inputs = [slots, lengths, queries, fresh] + ([spread] if plan["own"] else [])
-    in_specs = [smem, smem, vmem, vmem] + (
-        [pl.BlockSpec(memory_space=pltpu.HBM)] if plan["own"] else []
-    )
+    inputs = [slots, lengths, queries, fresh]
+    in_specs = [smem, smem, vmem, vmem]
     inside = [*operands, *(probs[group, l] for l in plan["given_probs"])]
     inside += [sums[name] for name in plan["sums_in"]]
     inputs += inside
@@ -256,17 +244,19 @@
     if plan["final"]:
         out_shape.append(jax.ShapeDtypeStruct((layers, heads * per_head, depth), jnp.bfloat16))
     count = len(units)
-    own_shape = (count, *spread.shape[3:]) if plan["own"] else (1, 1, 1, PAGE, depth)
+    out_specs = [anywhere] + [vmem] * (len(out_shape) - 1)
+    if plan["final"]:
+        out_specs[-1] = anywhere
     results = list(pl.pallas_call(
         functools.partial(head_kernel, plan),
         out_shape=out_shape,
         in_specs=in_specs,
-        out_specs=[anywhere] + [vmem] * (len(out_shape) - 1),
+        out_specs=out_specs,
         scratch_shapes=[
             pltpu.VMEM((ranks, per_head, blocks * PAGE), jnp.float32),
             pltpu.VMEM((count, ranks * blocks, PAGE, depth), jnp.bfloat16),
-            pltpu.VMEM(own_shape, jnp.bfloat16),
-            pltpu.SemaphoreType.DMA((count,)),
+            pltpu.VMEM((layers, heads * per_head, depth), jnp.bfloat16),
+            pltpu.SemaphoreType.DMA,
             pltpu.SemaphoreType.DMA((count,)),
         ],
         input_output_aliases=aliases,
@@ -300,20 +290,21 @@
     spread = spread_heads(kv_prefill, fanout)
     spread = spread.reshape(2, layers, spread.shape[2], fanout, blocks, PAGE, depth)
     units = [(k, l) for k in (0, 1) for l in range(layers)]
-    quarter = max(1, blocks // 4)
+    head_span = max(1, blocks // 4)
+    tail_span = max(1, blocks // 8)
     far = range(sources, seq_ranks)
 
     sends = []
     for k, l in units:
         spans = [(0, blocks)]
         if (k, l) == units[0]:
-            spans = [(0, quarter), (quarter, blocks)]
+            spans = [(0, head_span), (head_span, blocks)]
         elif (k, l) == units[-1]:
-            spans = [(0, blocks - quarter), (blocks - quarter, blocks)]
+            spans = [(0, blocks - tail_span), (blocks - tail_span, blocks)]
         for lo, hi in spans:
             stage = 0 if (k, l) == units[0] and lo == 0 else 1
             sends += [(stage, delta, [(k, l, lo, hi)]) for delta in far]
-    sends += [(2, delta, [(k, l, 0, blocks) for k, l in units]) for delta in range(1, sources)]
+    sends += [(2, delta, [(k, l, 0, blocks) for k, l in units]) for delta in range(sources)]
     arrived = []
     after = []
     for stage in range(3):
@@ -321,31 +312,33 @@
         if not batch:
             continue
         wanted = [[(k, l, delta, lo, hi) for k, l, lo, hi in items] for delta, items in batch]
-        blocks_out = cut(spread, wanted, after)
+        room = (11 << 20, 15 << 20, 24 << 20)[stage]
+        blocks_out = cut(spread, wanted, after, room)
         after = [blocks_out[0]]
         for (delta, items), block in zip(batch, blocks_out):
-            arrived.append((delta, items, swapped(block, "seq", delta)))
+            moved = swapped(block, "seq", delta) if delta > 0 else block
+            arrived.append((delta, items, moved))
 
     grouped = queries.reshape(layers, heads, queries.shape[2] // heads, depth)
-    args = (page_slots, lengths, grouped, new_kv, spread)
+    args = (page_slots, lengths, grouped, new_kv)
     pool_shape = (2, layers, heads, pages, PAGE, depth)
     probs, sums = {}, {}
 
-    def launch(units, group, chosen, pool, own=False, final=False, close=False):
+    def launch(units, group, chosen, pool, final=False, close=False):
         parts = [
             (at, row, (k, l), delta - group * sources, lo, hi)
             for at, (delta, items, _) in enumerate(chosen)
             for row, (k, l, lo, hi) in enumerate(items)
         ]
         plan = dict(
-            units=units, group=group, sources=sources, parts=parts, own=own, final=final,
-            close=close, tp_ranks=tp_ranks,
+            units=units, group=group, sources=sources, parts=parts, final=final,
+            close=close, tp_ranks=tp_ranks, piece=spread.shape[3:],
         )
         operands = [block for _, _, block in chosen]
         return head_call(plan, args, operands, probs, sums, pool, pool_shape)
 
     near = [a for a in arrived if a[0] < sources]
-    pool, out = launch(units, 0, near, None, own=True, final=heads == 1)
+    pool, out = launch(units, 0, near, None, final=heads == 1)
     for group in range(1, heads):
         for unit in units:
             chosen = [a for a in arrived if a[0] // sources == group and a[1][0][:2] == unit]

time: 102 us -> 102 us (level)
  local copies, waits for them, and re-layouts: 3.41 us -> 1.61 us
  Pallas kernels: 18.3 us -> 19.6 us
  starting transfers between devices: 14.8 us -> 16 us
    pallas_call x3, Pallas kernels: 1.86 us -> 3.88 us  [cut(): pl.pallas_call(functools.partial(cut_kernel, wanted), out_shape=shapes, i...]
    unnamed x12 -> x18, local copies, waits for them, and re-layouts: 3.41 us -> 1.61 us
    ppermute x13, starting transfers between devices: 14.8 us -> 16 us  [swapped(): lax.ppermute(array, axis, [(i, i ^ bits) for i in range(lax.axis_size(axi...]
  transfers between devices with their start and end apart: 13 -> 13, of which waited for: 11 -> 8; matrix products, arithmetic and copies ran while one was open for 0% -> 0% of each run, Pallas kernels for 14% -> 14%
where the time goes in v2:
time: 102 us
  waiting for transfers between devices  63 us (62%)
  Pallas kernels  19.6 us (19%)
  starting transfers between devices  16 us (16%)
  local copies, waits for them, and re-layouts  1.61 us (2%)
  between operations  1.45 us (1%)
    ppermute x13, waiting for transfers between devices, swapped(): lax.ppermute(array, axis, [(i, i ^ bits) for i in range(lax.axis_size(axi...  63 us
    ppermute x13, starting transfers between devices, swapped(): lax.ppermute(array, axis, [(i, i ^ bits) for i in range(lax.axis_size(axi...  16 us
    pallas_call x6, Pallas kernels, head_call(): pl.pallas_call(functools.partial(head_kernel, plan), out_shape=out_shape,...  15.7 us
    pallas_call x3, Pallas kernels, cut(): pl.pallas_call(functools.partial(cut_kernel, wanted), out_shape=shapes, i...  3.88 us
  transfers between devices with their start and end apart: 13, of which 8 were waited for; matrix products, arithmetic and copies ran while one was open for 0% of the time, Pallas kernels for 14%

profile of v2, /device:TPU:0, one launch (start us, length us, event | category | flops | bytes accessed | tf_op | source)
XLA Modules:
  0.0 101.6 jit_solution(156703972383095250)
XLA Ops:
  0.6 0.0 slice-start
  0.6 1.1 %shard_map.68 = (bf16[1,1,32,16,128]{4,3,2,1,0:T(8,128)(2,1)S(1)}, bf16[1,1,32,16,128]{4,3,2,1,0:T(8,128)(2,1)S(1)}) custom-call(bf16[2,2,4,1,128,16,128]{6,5,4,3,2,1,0:T(8,128)(2,1)} %bitcast.5), custom_call_target="tpu_custom_call" | custom-call | bytes 524288 | tf_op jit(solution)/shard_map/pallas_call | solution.py:51
  1.8 2.4 %shard_map.69 = (bf16[1,1,96,16,128]{4,3,2,1,0:T(8,128)(2,1)S(1)}, bf16[1,1,96,16,128]{4,3,2,1,0:T(8,128)(2,1)S(1)}, bf16[1,1,128,16,128]{4,3,2,1,0:T(8,128)(2,1...) custom-call(bf16[2,2,4,1,128,16,128]{6,5,4,3,2,1,0:T(8,128)(2,1)} %b, ...), custom_call_target="tpu_custom_call" | custom-call | bytes 7864320 | tf_op jit(solution)/shard_map/pallas_call | solution.py:51
  4.2 0.8 copy-done.3
  5.0 0.8 copy-done.5
  5.8 0.0 slice-done.1
  5.8 0.4 shard_map.70
  6.2 0.6 collective-permute-start.8
  6.7 2.6 %collective-permute-start.5 = (bf16[1,1,32,16,128]{4,3,2,1,0:T(8,128)(2,1)S(1)}, bf16[1,1,32,16,128]{4,3,2,1,0:T(8,128)(2,1)S(1)}, u32[]{:S(2)}, u32[]{:S(2)}) collective-permute-start(bf16[1,1,32,16,128]{4,3,2,1,0:T(8,128)(2,1)S(1)} %get-tuple-element.34), channel_id=1, source_target_pairs={{0,3},{1,2},{2,1},{3,0},{4,7},{5,6},{6,5},{7,4},{8,11},{9,10},{10,... | collective-permute-start | bytes 393224 | tf_op jit(solution)/shard_map/ppermute | solution.py:18
  9.3 0.0 collective-permute-start.4
  9.4 2.0 %collective-permute-start.2 = (bf16[1,1,128,16,128]{4,3,2,1,0:T(8,128)(2,1)S(1)}, bf16[1,1,128,16,128]{4,3,2,1,0:T(8,128)(2,1)S(1)}, u32[]{:S(2)}, u32[]{:S(2)}) collective-permute-start(bf16[1,1,128,16,128]{4,3,2,1,0:T(8,128)(2,1)S(1)} %get-tuple-element.32), channel_id=1, source_target_pairs={{0,2},{1,3},{2,0},{3,1},{4,6},{5,7},{6,4},{7,5},{8,10},{9,11},{10,... | collective-permute-start | bytes 1572872 | tf_op jit(solution)/shard_map/ppermute | solution.py:18
  11.4 1.9 %collective-permute-done.5.refs_5_ = bf16[1,1,32,16,128]{4,3,2,1,0:T(8,128)(2,1)S(1)} collective-permute-done((bf16[1,1,32,16,128]{4,3,2,1,0:T(8,128)(2,1)S(1)}, bf16[1,1,32,16,128]{4,3,2,1,0:T(8,128)(2,1)S(1)}, u32[]{:S(2)}, u32[]{:S(2)}) %collective-permute-start.5) | collective-permute-done | bytes 131104 | tf_op jit(solution)/shard_map/ppermute | solution.py:18
  13.2 1.9 %collective-permute-start.7 = (bf16[1,1,96,16,128]{4,3,2,1,0:T(8,128)(2,1)S(1)}, bf16[1,1,96,16,128]{4,3,2,1,0:T(8,128)(2,1)S(1)}, u32[]{:S(2)}, u32[]{:S(2)}) collective-permute-start(bf16[1,1,96,16,128]{4,3,2,1,0:T(8,128)(2,1)S(1)} %copy-done.6), channel_id=1, source_target_pairs={{0,3},{1,2},{2,1},{3,0},{4,7},{5,6},{6,5},{7,4},{8,11},{9,10},{10,... | collective-permute-start | bytes 1179656 | tf_op jit(solution)/shard_map/ppermute | solution.py:18
  15.1 1.3 %collective-permute-done.4.refs_4_ = bf16[1,1,32,16,128]{4,3,2,1,0:T(8,128)(2,1)S(1)} collective-permute-done((bf16[1,1,32,16,128]{4,3,2,1,0:T(8,128)(2,1)S(1)}, bf16[1,1,32,16,128]{4,3,2,1,0:T(8,128)(2,1)S(1)}, u32[]{:S(2)}, u32[]{:S(2)}) %collective-permute-start.4) | collective-permute-done | bytes 131104 | tf_op jit(solution)/shard_map/ppermute | solution.py:18
  16.4 2.1 %collective-permute-start.6 = (bf16[1,1,96,16,128]{4,3,2,1,0:T(8,128)(2,1)S(1)}, bf16[1,1,96,16,128]{4,3,2,1,0:T(8,128)(2,1)S(1)}, u32[]{:S(2)}, u32[]{:S(2)}) collective-permute-start(bf16[1,1,96,16,128]{4,3,2,1,0:T(8,128)(2,1)S(1)} %get-tuple-element.35.refs_1_), channel_id=1, source_target_pairs={{0,2},{1,3},{2,0},{3,1},{4,6},{5,7},{6,4},{7,5},{8,10},{9,11},{10,... | collective-permute-start | bytes 1179656 | tf_op jit(solution)/shard_map/ppermute | solution.py:18
  18.5 28.4 %collective-permute-done.7.refs_7_ = bf16[1,1,96,16,128]{4,3,2,1,0:T(8,128)(2,1)S(1)} collective-permute-done((bf16[1,1,96,16,128]{4,3,2,1,0:T(8,128)(2,1)S(1)}, bf16[1,1,96,16,128]{4,3,2,1,0:T(8,128)(2,1)S(1)}, u32[]{:S(2)}, u32[]{:S(2)}) %collective-permute-start.7) | collective-permute-done | bytes 393248 | tf_op jit(solution)/shard_map/ppermute | solution.py:18
  46.9 1.3 %collective-permute-start.9 = (bf16[1,1,128,16,128]{4,3,2,1,0:T(8,128)(2,1)S(1)}, bf16[1,1,128,16,128]{4,3,2,1,0:T(8,128)(2,1)S(1)}, u32[]{:S(2)}, u32[]{:S(2)}) collective-permute-start(bf16[1,1,128,16,128]{4,3,2,1,0:T(8,128)(2,1)S(1)} %get-tuple-element.44), channel_id=1, source_target_pairs={{0,2},{1,3},{2,0},{3,1},{4,6},{5,7},{6,4},{7,5},{8,10},{9,11},{10,... | collective-permute-start | bytes 1572872 | tf_op jit(solution)/shard_map/ppermute | solution.py:18
  48.2 7.6 %collective-permute-done.6.refs_6_ = bf16[1,1,96,16,128]{4,3,2,1,0:T(8,128)(2,1)S(1)} collective-permute-done((bf16[1,1,96,16,128]{4,3,2,1,0:T(8,128)(2,1)S(1)}, bf16[1,1,96,16,128]{4,3,2,1,0:T(8,128)(2,1)S(1)}, u32[]{:S(2)}, u32[]{:S(2)}) %collective-permute-start.6) | collective-permute-done | bytes 393248 | tf_op jit(solution)/shard_map/ppermute | solution.py:18
  55.8 0.6 collective-permute-start.10
  56.3 1.6 %collective-permute-start.11 = (bf16[1,1,112,16,128]{4,3,2,1,0:T(8,128)(2,1)S(1)}, bf16[1,1,112,16,128]{4,3,2,1,0:T(8,128)(2,1)S(1)}, u32[]{:S(2)}, u32[]{:S(2)}) collective-permute-start(bf16[1,1,112,16,128]{4,3,2,1,0:T(8,128)(2,1)S(1)} %copy-done.4), channel_id=1, source_target_pairs={{0,2},{1,3},{2,0},{3,1},{4,6},{5,7},{6,4},{7,5},{8,10},{9,11},{10,... | collective-permute-start | bytes 1376264 | tf_op jit(solution)/shard_map/ppermute | solution.py:18
  57.9 1.4 %collective-permute-start.12 = (bf16[1,1,112,16,128]{4,3,2,1,0:T(8,128)(2,1)S(1)}, bf16[1,1,112,16,128]{4,3,2,1,0:T(8,128)(2,1)S(1)}, u32[]{:S(2)}, u32[]{:S(2)}) collective-permute-start(bf16[1,1,112,16,128]{4,3,2,1,0:T(8,128)(2,1)S(1)} %get-tuple-element.50), channel_id=1, source_target_pairs={{0,3},{1,2},{2,1},{3,0},{4,7},{5,6},{6,5},{7,4},{8,11},{9,10},{10,... | collective-permute-start | bytes 1376264 | tf_op jit(solution)/shard_map/ppermute | solution.py:18
  59.3 7.7 %collective-permute-done.9.refs_4_ = bf16[1,1,128,16,128]{4,3,2,1,0:T(8,128)(2,1)S(1)} collective-permute-done((bf16[1,1,128,16,128]{4,3,2,1,0:T(8,128)(2,1)S(1)}, bf16[1,1,128,16,128]{4,3,2,1,0:T(8,128)(2,1)S(1)}, u32[]{:S(2)}, u32[]{:S(2)}) %collective-permute-start.9) | collective-permute-done | bytes 524320 | tf_op jit(solution)/shard_map/ppermute | solution.py:18
  67.0 2.1 %collective-permute-start = (bf16[1,1,16,16,128]{4,3,2,1,0:T(8,128)(2,1)S(1)}, bf16[1,1,16,16,128]{4,3,2,1,0:T(8,128)(2,1)S(1)}, u32[]{:S(2)}, u32[]{:S(2)}) collective-permute-start(bf16[1,1,16,16,128]{4,3,2,1,0:T(8,128)(2,1)S(1)} %get-tuple-element.30), channel_id=1, source_target_pairs={{0,2},{1,3},{2,0},{3,1},{4,6},{5,7},{6,4},{7,5},{8,10},{9,11},{10,... | collective-permute-start | bytes 196616 | tf_op jit(solution)/shard_map/ppermute | solution.py:18
  69.8 5.4 %shard_map.71 = (bf16[2,2,2,256,16,128]{5,4,3,2,1,0:T(8,128)(2,1)}, bf16[2,8,2048]{2,1,0:T(8,128)(2,1)}, bf16[2,8,2048]{2,1,0:T(8,128)(2,1)}, f32[8,128]{1,0:T(8,128)S(1)}, f32[8,128]{1,0:T(8,128)S(1)}) custom-call(s32[1,256]{1,0:T(1,128)S(1)} %copy-done.2, s32[1]{0:T(128)S(6)} %copy.18.refs_1_, bf16[2,2,8,128]{3,2,1,0:T(8,128)(2,1)S(1)} %bitcast.10, ...), custom_call_target="tpu_custom_call" | custom-call | bytes 16777216 | tf_op jit(solution)/shard_map/pallas_call | solution.py:250
  75.1 2.5 %shard_map.72 = (bf16[2,2,2,256,16,128]{5,4,3,2,1,0:T(8,128)(2,1)}, bf16[2,8,2048]{2,1,0:T(8,128)(2,1)S(1)}) custom-call(s32[1,256]{1,0:T(1,128)S(1)} %copy-done.2, s32[1]{0:T(128)S(6)} %copy.18.refs_1_, bf16[2,2,8,128]{3,2,1,0:T(8,128)(2,1)S(1)} %bitcast.11, bf16[2,2,1,8,128]{4,3,2,1,0:T(8,128)(2,1)S(1)} %copy-done.1, ...), custom_call_target="tpu_custom_call", output_to_operand_aliasing={{0}: (8, {})} | custom-call | bytes 4194304 | tf_op jit(solution)/shard_map/pallas_call | solution.py:250
  77.6 2.5 %shard_map.73 = (bf16[2,2,2,256,16,128]{5,4,3,2,1,0:T(8,128)(2,1)}, bf16[2,8,2048]{2,1,0:T(8,128)(2,1)S(1)}) custom-call(s32[1,256]{1,0:T(1,128)S(1)} %copy-done.2, s32[1]{0:T(128)S(6)} %copy.18.refs_1_, bf16[2,2,8,128]{3,2,1,0:T(8,128)(2,1)S(1)} %bitcast.12, bf16[2,2,1,8,128]{4,3,2,1,0:T(8,128)(2,1)S(1)} %copy-done.1, ...), custom_call_target="tpu_custom_call", output_to_operand_aliasing={{0}: (6, {})} | custom-call | bytes 4194304 | tf_op jit(solution)/shard_map/pallas_call | solution.py:250
  80.0 2.1 %shard_map.74 = (bf16[2,2,2,256,16,128]{5,4,3,2,1,0:T(8,128)(2,1)}, f32[8,128]{1,0:T(8,128)S(1)}) custom-call(s32[1,256]{1,0:T(1,128)S(1)} %copy-done.2, s32[1]{0:T(128)S(6)} %copy.18.refs_1_, bf16[2,2,8,128]{3,2,1,0:T(8,128)(2,1)S(1)} %bitcast.13, bf16[2,2,1,8,128]{4,3,2,1,0:T(8,128)(2,1)S(1)} %copy-done.1, ...), custom_call_target="tpu_custom_call", output_to_operand_aliasing={{0}: (7, {})} | custom-call | bytes 4194304 | tf_op jit(solution)/shard_map/pallas_call | solution.py:250
  82.1 6.0 %collective-permute-done.11.refs_4_ = bf16[1,1,112,16,128]{4,3,2,1,0:T(8,128)(2,1)S(1)} collective-permute-done((bf16[1,1,112,16,128]{4,3,2,1,0:T(8,128)(2,1)S(1)}, bf16[1,1,112,16,128]{4,3,2,1,0:T(8,128)(2,1)S(1)}, u32[]{:S(2)}, u32[]{:S(2)}) %collective-permute-start.11) | collective-permute-done | bytes 458784 | tf_op jit(solution)/shard_map/ppermute | solution.py:18
  88.1 9.4 %collective-permute-done.12.refs_5_ = bf16[1,1,112,16,128]{4,3,2,1,0:T(8,128)(2,1)S(1)} collective-permute-done((bf16[1,1,112,16,128]{4,3,2,1,0:T(8,128)(2,1)S(1)}, bf16[1,1,112,16,128]{4,3,2,1,0:T(8,128)(2,1)S(1)}, u32[]{:S(2)}, u32[]{:S(2)}) %collective-permute-start.12) | collective-permute-done | bytes 458784 | tf_op jit(solution)/shard_map/ppermute | solution.py:18
  97.5 2.0 %shard_map.75 = (bf16[2,2,2,256,16,128]{5,4,3,2,1,0:T(8,128)(2,1)}, f32[8,128]{1,0:T(8,128)S(1)}) custom-call(s32[1,256]{1,0:T(1,128)S(1)} %copy-done.2, s32[1]{0:T(128)S(6)} %copy.18.refs_1_, bf16[2,2,8,128]{3,2,1,0:T(8,128)(2,1)S(1)} %bitcast.14, bf16[2,2,1,8,128]{4,3,2,1,0:T(8,128)(2,1)S(1)} %copy-done.1, ...), custom_call_target="tpu_custom_call", output_to_operand_aliasing={{0}: (7, {})} | custom-call | bytes 4194304 | tf_op jit(solution)/shard_map/pallas_call | solution.py:250
  99.5 0.7 collective-permute-done.1.refs_5_
  100.2 1.4 %shard_map.76 = (bf16[2,2,2,256,16,128]{5,4,3,2,1,0:T(8,128)(2,1)}, bf16[2,16,128]{2,1,0:T(8,128)(2,1)}) custom-call(s32[1,256]{1,0:T(1,128)S(1)} %copy-done.2, s32[1]{0:T(128)S(6)} %copy.18.refs_1_, bf16[2,2,8,128]{3,2,1,0:T(8,128)(2,1)S(1)} %bitcast.15, bf16[2,2,1,8,128]{4,3,2,1,0:T(8,128)(2,1)S(1)} %copy-done.1, ...), custom_call_target="tpu_custom_call", output_to_operand_aliasing={{0}: (11, {})} | custom-call | bytes 4194304 | tf_op jit(solution)/shard_map/pallas_call | solution.py:250
  (22 shorter events, 0.1 us)
Async XLA Ops:
  0.6 5.1 %slice-start = ((s8[8388608]{0:T(1024)(128)(4,1)}), s8[4194304]{0:T(1024)(128)(4,1)S(1)}, s32[]{:S(2)}) async-start(s8[8388608]{0:T(1024)(128)(4,1)} %bitcast.7), calls=%async_computation | async-start | bytes 8388608
  1.8 4.0 %slice-start.1 = ((s8[8388608]{0:T(1024)(128)(4,1)}), s8[4194304]{0:T(1024)(128)(4,1)S(1)}, s32[]{:S(2)}) async-start(s8[8388608]{0:T(1024)(128)(4,1)} %bitcast.7), calls=%async_computation.1 | async-start | bytes 8388608
  1.8 67.9 %copy-start = (bf16[2,1,16,128]{3,2,1,0:T(8,128)(2,1)S(1)}, bf16[2,1,16,128]{3,2,1,0:T(8,128)(2,1)}, u32[]{:S(2)}) copy-start(bf16[2,1,16,128]{3,2,1,0:T(8,128)(2,1)} %param.6) | copy-start | bytes 24580
  1.8 67.9 %copy-start.1 = (bf16[2,2,1,8,128]{4,3,2,1,0:T(8,128)(2,1)S(1)}, bf16[2,2,1,8,128]{4,3,2,1,0:T(8,128)(2,1)}, u32[]{:S(2)}) copy-start(bf16[2,2,1,8,128]{4,3,2,1,0:T(8,128)(2,1)} %refs_3_.11) | copy-start | bytes 24580
  1.8 67.9 %copy-start.2 = (s32[1,256]{1,0:T(1,128)S(1)}, s32[1,256]{1,0:T(1,128)}, u32[]{:S(2)}) copy-start(s32[1,256]{1,0:T(1,128)} %refs_0_.11) | copy-start | bytes 3076
  4.2 0.8 copy-start.3
  5.0 0.8 copy-start.5
  5.8 7.4 %copy-start.6 = (bf16[1,1,96,16,128]{4,3,2,1,0:T(8,128)(2,1)S(1)}, bf16[1,1,96,16,128]{4,3,2,1,0:T(8,128)(2,1)}, u32[]{:S(2)}) copy-start(bf16[1,1,96,16,128]{4,3,2,1,0:T(8,128)(2,1)} %copy-done.5) | copy-start | bytes 1179652
  5.8 50.5 %copy-start.4 = (bf16[1,1,112,16,128]{4,3,2,1,0:T(8,128)(2,1)S(1)}, bf16[1,1,112,16,128]{4,3,2,1,0:T(8,128)(2,1)}, u32[]{:S(2)}) copy-start(bf16[1,1,112,16,128]{4,3,2,1,0:T(8,128)(2,1)} %copy-done.3) | copy-start | bytes 1376260
  6.2 62.9 %collective-permute-start.8 = (bf16[4,1,128,16,128]{4,3,2,1,0:T(8,128)(2,1)S(1)}, bf16[4,1,128,16,128]{4,3,2,1,0:T(8,128)(2,1)S(1)}, u32[]{:S(2)}, u32[]{:S(2)}) collective-permute-start(bf16[4,1,128,16,128]{4,3,2,1,0:T(8,128)(2,1)S(1)} %get-tuple-element.38), channel_id=1, source_target_pairs={{0,1},{1,0},{2,3},{3,2},{4,5},{5,4},{6,7},{7,6},{8,9},{9,8},{10,11... | collective-permute-start | bytes 6291464 | tf_op jit(solution)/shard_map/ppermute | solution.py:18
  6.7 6.5 %collective-permute-start.5 = (bf16[1,1,32,16,128]{4,3,2,1,0:T(8,128)(2,1)S(1)}, bf16[1,1,32,16,128]{4,3,2,1,0:T(8,128)(2,1)S(1)}, u32[]{:S(2)}, u32[]{:S(2)}) collective-permute-start(bf16[1,1,32,16,128]{4,3,2,1,0:T(8,128)(2,1)S(1)} %get-tuple-element.34), channel_id=1, source_target_pairs={{0,3},{1,2},{2,1},{3,0},{4,7},{5,6},{6,5},{7,4},{8,11},{9,10},{10,... | collective-permute-start | bytes 393224 | tf_op jit(solution)/shard_map/ppermute | solution.py:18
  9.3 7.1 %collective-permute-start.4 = (bf16[1,1,32,16,128]{4,3,2,1,0:T(8,128)(2,1)S(1)}, bf16[1,1,32,16,128]{4,3,2,1,0:T(8,128)(2,1)S(1)}, u32[]{:S(2)}, u32[]{:S(2)}) collective-permute-start(bf16[1,1,32,16,128]{4,3,2,1,0:T(8,128)(2,1)S(1)} %get-tuple-element.29.refs_1_), channel_id=1, source_target_pairs={{0,2},{1,3},{2,0},{3,1},{4,6},{5,7},{6,4},{7,5},{8,10},{9,11},{10,... | collective-permute-start | bytes 393224 | tf_op jit(solution)/shard_map/ppermute | solution.py:18
  9.4 47.0 %collective-permute-start.2 = (bf16[1,1,128,16,128]{4,3,2,1,0:T(8,128)(2,1)S(1)}, bf16[1,1,128,16,128]{4,3,2,1,0:T(8,128)(2,1)S(1)}, u32[]{:S(2)}, u32[]{:S(2)}) collective-permute-start(bf16[1,1,128,16,128]{4,3,2,1,0:T(8,128)(2,1)S(1)} %get-tuple-element.32), channel_id=1, source_target_pairs={{0,2},{1,3},{2,0},{3,1},{4,6},{5,7},{6,4},{7,5},{8,10},{9,11},{10,... | collective-permute-start | bytes 1572872 | tf_op jit(solution)/shard_map/ppermute | solution.py:18
  11.4 46.6 %collective-permute-start.3 = (bf16[1,1,128,16,128]{4,3,2,1,0:T(8,128)(2,1)S(1)}, bf16[1,1,128,16,128]{4,3,2,1,0:T(8,128)(2,1)S(1)}, u32[]{:S(2)}, u32[]{:S(2)}) collective-permute-start(bf16[1,1,128,16,128]{4,3,2,1,0:T(8,128)(2,1)S(1)} %get-tuple-element.33), channel_id=1, source_target_pairs={{0,3},{1,2},{2,1},{3,0},{4,7},{5,6},{6,5},{7,4},{8,11},{9,10},{10,... | collective-permute-start | bytes 1572872 | tf_op jit(solution)/shard_map/ppermute | solution.py:18
  13.2 33.7 %collective-permute-start.7 = (bf16[1,1,96,16,128]{4,3,2,1,0:T(8,128)(2,1)S(1)}, bf16[1,1,96,16,128]{4,3,2,1,0:T(8,128)(2,1)S(1)}, u32[]{:S(2)}, u32[]{:S(2)}) collective-permute-start(bf16[1,1,96,16,128]{4,3,2,1,0:T(8,128)(2,1)S(1)} %copy-done.6), channel_id=1, source_target_pairs={{0,3},{1,2},{2,1},{3,0},{4,7},{5,6},{6,5},{7,4},{8,11},{9,10},{10,... | collective-permute-start | bytes 1179656 | tf_op jit(solution)/shard_map/ppermute | solution.py:18
  16.4 39.3 %collective-permute-start.6 = (bf16[1,1,96,16,128]{4,3,2,1,0:T(8,128)(2,1)S(1)}, bf16[1,1,96,16,128]{4,3,2,1,0:T(8,128)(2,1)S(1)}, u32[]{:S(2)}, u32[]{:S(2)}) collective-permute-start(bf16[1,1,96,16,128]{4,3,2,1,0:T(8,128)(2,1)S(1)} %get-tuple-element.35.refs_1_), channel_id=1, source_target_pairs={{0,2},{1,3},{2,0},{3,1},{4,6},{5,7},{6,4},{7,5},{8,10},{9,11},{10,... | collective-permute-start | bytes 1179656 | tf_op jit(solution)/shard_map/ppermute | solution.py:18
  46.9 20.1 %collective-permute-start.9 = (bf16[1,1,128,16,128]{4,3,2,1,0:T(8,128)(2,1)S(1)}, bf16[1,1,128,16,128]{4,3,2,1,0:T(8,128)(2,1)S(1)}, u32[]{:S(2)}, u32[]{:S(2)}) collective-permute-start(bf16[1,1,128,16,128]{4,3,2,1,0:T(8,128)(2,1)S(1)} %get-tuple-element.44), channel_id=1, source_target_pairs={{0,2},{1,3},{2,0},{3,1},{4,6},{5,7},{6,4},{7,5},{8,10},{9,11},{10,... | collective-permute-start | bytes 1572872 | tf_op jit(solution)/shard_map/ppermute | solution.py:18
  55.8 24.3 %collective-permute-start.10 = (bf16[1,1,128,16,128]{4,3,2,1,0:T(8,128)(2,1)S(1)}, bf16[1,1,128,16,128]{4,3,2,1,0:T(8,128)(2,1)S(1)}, u32[]{:S(2)}, u32[]{:S(2)}) collective-permute-start(bf16[1,1,128,16,128]{4,3,2,1,0:T(8,128)(2,1)S(1)} %get-tuple-element.45), channel_id=1, source_target_pairs={{0,3},{1,2},{2,1},{3,0},{4,7},{5,6},{6,5},{7,4},{8,11},{9,10},{10,... | collective-permute-start | bytes 1572872 | tf_op jit(solution)/shard_map/ppermute | solution.py:18
  56.3 31.7 %collective-permute-start.11 = (bf16[1,1,112,16,128]{4,3,2,1,0:T(8,128)(2,1)S(1)}, bf16[1,1,112,16,128]{4,3,2,1,0:T(8,128)(2,1)S(1)}, u32[]{:S(2)}, u32[]{:S(2)}) collective-permute-start(bf16[1,1,112,16,128]{4,3,2,1,0:T(8,128)(2,1)S(1)} %copy-done.4), channel_id=1, source_target_pairs={{0,2},{1,3},{2,0},{3,1},{4,6},{5,7},{6,4},{7,5},{8,10},{9,11},{10,... | collective-permute-start | bytes 1376264 | tf_op jit(solution)/shard_map/ppermute | solution.py:18
  57.9 39.6 %collective-permute-start.12 = (bf16[1,1,112,16,128]{4,3,2,1,0:T(8,128)(2,1)S(1)}, bf16[1,1,112,16,128]{4,3,2,1,0:T(8,128)(2,1)S(1)}, u32[]{:S(2)}, u32[]{:S(2)}) collective-permute-start(bf16[1,1,112,16,128]{4,3,2,1,0:T(8,128)(2,1)S(1)} %get-tuple-element.50), channel_id=1, source_target_pairs={{0,3},{1,2},{2,1},{3,0},{4,7},{5,6},{6,5},{7,4},{8,11},{9,10},{10,... | collective-permute-start | bytes 1376264 | tf_op jit(solution)/shard_map/ppermute | solution.py:18
  67.0 32.5 %collective-permute-start = (bf16[1,1,16,16,128]{4,3,2,1,0:T(8,128)(2,1)S(1)}, bf16[1,1,16,16,128]{4,3,2,1,0:T(8,128)(2,1)S(1)}, u32[]{:S(2)}, u32[]{:S(2)}) collective-permute-start(bf16[1,1,16,16,128]{4,3,2,1,0:T(8,128)(2,1)S(1)} %get-tuple-element.30), channel_id=1, source_target_pairs={{0,2},{1,3},{2,0},{3,1},{4,6},{5,7},{6,4},{7,5},{8,10},{9,11},{10,... | collective-permute-start | bytes 196616 | tf_op jit(solution)/shard_map/ppermute | solution.py:18
  69.1 31.1 %collective-permute-start.1 = (bf16[1,1,16,16,128]{4,3,2,1,0:T(8,128)(2,1)S(1)}, bf16[1,1,16,16,128]{4,3,2,1,0:T(8,128)(2,1)S(1)}, u32[]{:S(2)}, u32[]{:S(2)}) collective-permute-start(bf16[1,1,16,16,128]{4,3,2,1,0:T(8,128)(2,1)S(1)} %get-tuple-element.31), channel_id=1, source_target_pairs={{0,3},{1,2},{2,1},{3,0},{4,7},{5,6},{6,5},{7,4},{8,11},{9,10},{10,... | collective-permute-start | bytes 196616 | tf_op jit(solution)/shard_map/ppermute | solution.py:18
